TPU v7x, 32 devices: a whole 2x2x4 slice. The times are simulated.
32 devices in a mesh: slab: 8 (over z, y), layer: 4 (over x, core).
Axes of the slice: x: 2, y: 2, z: 4, core: 2. Of those that a mesh axis runs over, the one named last changes fastest.
Arguments:
- hamilton_blocks: bfloat16 [128, 128, 128], P(('slab', 'layer')), may hold values from -0.25 to 0.25
- pair_ids: int32 [32, 10], P(('slab', 'layer')), may hold values from 0 to 127, as said below
- weights: float32 [32, 10], P(('slab', 'layer')), may hold values from 0.25 to 4
- potential: float32 [1], replicated, may hold values from -1 to 1
Outputs:
- density: float32 [128, 128, 128], P(('slab', 'layer'))
- energy: float32 [128, 128, 128], P(('slab', 'layer'))
Inputs may be any that keep to these rules, and one draw needn't show every extreme that they name: `pair_ids`: the entries of one row are distinct. Slot p is owned by device p // 4, whose slab index is that device // 4 and layer index that device % 4. Row d names only slots owned by devices whose slab index is that of device d, or one more or one less cyclically over 8, with any layer index. A row names at most 4 slots of any one device, and exactly 4 of some device; in every draw some device has exactly 4 of its slots named by each of the 3 * 4 rows that may name its slots.
All inputs are finite; a program needn't handle non-finite values.
Results may differ from a plain program's by a relative error of at most 0.0017.
Values may be sent and summed in bfloat16 or wider, within the bound.
No kernel may reach another device: no remote copies, remote signals or barrier semaphores. Data moves between devices by JAX's collectives and lax.ppermute only.
A program may use at most 64 MiB of HBM per device.

v0:
```python
import functools

import jax
import jax.numpy as jnp
import numpy as np
from jax import lax
from jax.experimental import pallas as pl
from jax.experimental.pallas import tpu as pltpu
from jax.sharding import PartitionSpec as P


ITERS = 2
AXES = ("slab", "layer")


def block_order(pair_count):
    return (int(np.sqrt(8 * pair_count + 1)) - 1) // 2


def halves(value):
    high = value.astype(jnp.bfloat16)
    low = (value - high.astype(jnp.float32)).astype(jnp.bfloat16)
    return high, low


def mm(left, right):
    return jnp.dot(left, right, preferred_element_type=jnp.float32)


def step_kernel(sizes, *refs):
    slabs, groups, cores, pieces, rows, nb, bs = sizes
    ids, weights = refs[:rows], refs[rows : 2 * rows]
    potential, near, far, kept, sent = refs[2 * rows : 2 * rows + 5]
    scratch = refs[2 * rows + 5 :]
    per_row = len(scratch) // rows
    order = nb * bs
    wide = min(2 * bs, order)
    half_count = order // wide
    f32, bf16 = jnp.float32, jnp.bfloat16
    here_slab = lax.axis_index("slab")
    here_layer = lax.axis_index("layer")
    here_group, here_core = here_layer // cores, here_layer % cores
    mu = potential[0]
    pairs = [(a, b) for a in range(nb) for b in range(a, nb)]

    def eye(size, value):
        down = lax.broadcasted_iota(jnp.int32, (size, size), 0)
        return jnp.where(down == lax.broadcasted_iota(jnp.int32, (size, size), 1), value, 0.0)

    def strips():
        for i in range(half_count):
            for row in range(rows):
                yield i, row, pl.ds(i * wide, wide), pl.ds(i * wide, order - i * wide)

    def store_halves(high, low, upper, right, value):
        high[upper, right], low[upper, right] = halves(value)
        for j in range(right.start + wide, order, wide):
            part = pl.ds(j, wide)
            high[part, upper] = high[upper, part].T
            low[part, upper] = low[upper, part].T

    def eye_strip(right, value):
        down = lax.broadcasted_iota(jnp.int32, (wide, right.size), 0)
        return jnp.where(down == lax.broadcasted_iota(jnp.int32, (wide, right.size), 1), value, 0.0)

    def where_is(row, k):
        slot_id = ids[row][0, k]
        slot = slot_id % pieces
        device = slot_id // pieces
        layer = device % (groups * cores)
        offset = (device // (groups * cores) - here_slab + 1 + slabs) % slabs
        return offset, layer // cores, layer % cores, slot

    def cut(index):
        return pl.ds(index * bs, bs)

    def low_cut(index):
        part = index * bs % wide
        return index * bs // wide, pl.ds(part, bs), pl.ds(part, bs)

    spots = [[where_is(row, k) for k in range(len(pairs))] for row in range(rows)]
    state = [scratch[row * per_row : (row + 1) * per_row] for row in range(rows)]
    inverses = []

    for row in range(rows):
        base_hi, base_lo, diag_hi, diag_lo = state[row][:4]
        base_lo[...] = jnp.zeros_like(base_lo)
        squares = jnp.zeros((bs, bs), f32)
        for k, (a, b) in enumerate(pairs):
            offset, group, core, slot = spots[row][k]
            turn = (here_group - group + groups) % groups
            place = jnp.where(here_slab % 2 == 0, offset, 2 - offset)
            index = (turn * 3 + place) * pieces + slot
            block = near[index]
            if cores > 1:
                block = jnp.where(core == here_core, block, far[index])
            wide_block = block.astype(f32)
            if a == b:
                ham = wide_block + wide_block.T
                base = ham - eye(bs, mu)
                squares += base * base
                base_hi[cut(a), cut(a)], base_lo[low_cut(a)] = halves(base)
                diag_hi[a], diag_lo[a] = halves(ham)
            else:
                squares += 2.0 * (wide_block * wide_block)
                base_hi[cut(a), cut(b)] = block
                base_hi[cut(b), cut(a)] = block.T
        total = jnp.sum(squares, axis=(0, 1), keepdims=True)
        inverses.append(1.0 / (2.0 * jnp.sqrt(total / order + 1e-06)))

    for target in (kept, sent):
        target[...] = jnp.zeros_like(target)

    for i, row, upper, right in strips():
        base_hi, base_lo, _, _, _, _, b_hi, b_lo, _, _ = state[row]
        square = mm(base_hi[upper, :], base_hi[:, right]) + mm(base_lo[i], base_hi[upper, right])
        square += jnp.concatenate(
            [mm(base_hi[upper, pl.ds(j * wide, wide)], base_lo[j]) for j in range(i, half_count)],
            axis=1,
        )
        scale = 0.5 * inverses[row] * inverses[row]
        store_halves(b_hi, b_lo, upper, right, eye_strip(right, 1.5) - scale * square)
    for i, row, upper, right in strips():
        base_hi, base_lo, _, _, a_hi, a_lo, b_hi, b_lo, _, _ = state[row]
        value = mm(base_hi[upper, :], b_hi[:, right]) + mm(base_hi[upper, :], b_lo[:, right])
        value += mm(base_lo[i], b_hi[upper, right])
        store_halves(a_hi, a_lo, upper, right, -inverses[row] * value)
    for row in range(rows):
        base_hi, base_lo, diag_hi, diag_lo = state[row][:4]
        for a in range(nb):
            base_hi[cut(a), cut(a)] = diag_hi[a]
            base_lo[low_cut(a)] = diag_lo[a]
    for step in range(1, ITERS):
        for i, row, upper, right in strips():
            _, _, _, _, a_hi, a_lo, b_hi, b_lo, _, _ = state[row]
            square = mm(a_hi[upper, :], a_hi[:, right]) + mm(a_hi[upper, :], a_lo[:, right])
            square += mm(a_lo[upper, :], a_hi[:, right])
            store_halves(b_hi, b_lo, upper, right, eye_strip(right, 1.5) - 0.5 * square)
        for i, row, upper, right in strips():
            _, _, _, _, a_hi, a_lo, b_hi, b_lo, full, _ = state[row]
            value = mm(a_hi[upper, :], b_hi[:, right]) + mm(a_hi[upper, :], b_lo[:, right])
            value += mm(a_lo[upper, :], b_hi[:, right])
            if step == ITERS - 1:
                value = 0.5 * (eye_strip(right, 1.0) + value)
            full[upper, right] = value
        for i, row, upper, right in strips():
            _, _, _, _, a_hi, a_lo, _, _, full, _ = state[row]
            store_halves(a_hi, a_lo, upper, right, full[upper, right])
    for i, row, upper, right in strips():
        base_hi, base_lo, _, _, a_hi, a_lo, _, _, _, full2 = state[row]
        value = mm(a_hi[upper, :], base_hi[:, right]) + mm(a_lo[upper, :], base_hi[:, right])
        value += jnp.concatenate(
            [mm(a_hi[upper, pl.ds(j * wide, wide)], base_lo[j]) for j in range(i, half_count)],
            axis=1,
        )
        full2[upper, right] = value
    for row in range(rows):
        full, full2 = state[row][8:]
        for k, (a, b) in enumerate(pairs):
            offset, group, core, slot = spots[row][k]
            weight = weights[row][0, k]

            def add(target):
                at = offset * pieces + slot
                for mat, source in ((0, full), (1, full2)):
                    part = (weight * source[cut(a), cut(b)]).astype(bf16).astype(f32)
                    target[mat, at] = (target[mat, at].astype(f32) + part).astype(target.dtype)

            @pl.when(jnp.logical_and(group == here_group, core == here_core))
            def _():
                add(kept)

            if cores > 1:

                @pl.when(jnp.logical_and(group == here_group, core != here_core))
                def _():
                    add(sent)


def shards(hamilton_blocks, pair_ids, weights, potential):
    pieces, bs, _ = hamilton_blocks.shape
    slabs = lax.axis_size("slab")
    layers = lax.axis_size("layer")
    cores = 2 if layers % 2 == 0 else 1
    groups = layers // cores
    pair_count = pair_ids.shape[1]
    nb = block_order(pair_count)
    order = nb * bs
    wide = min(2 * bs, order)

    def send(value, slab_of, group_step=0, core_step=0):
        pairs = []
        for s in range(slabs):
            for g in range(groups):
                for c in range(cores):
                    there = (slab_of(s) % slabs * groups + (g + group_step) % groups) * cores
                    pairs.append(((s * groups + g) * cores + c, there + (c + core_step) % cores))
        return lax.ppermute(value, AXES, pairs)

    same = lambda s: s
    first = lambda s: s - 1 if s % 2 else s + 1
    second = lambda s: s + 1 if s % 2 else s - 1
    table = [send(hamilton_blocks, second), hamilton_blocks, send(hamilton_blocks, first)]
    for g in range(1, groups):
        table += [
            send(table[0], same, g), send(hamilton_blocks, same, g), send(hamilton_blocks, first, g)
        ]
    ids = [pair_ids] + [send(pair_ids, same, g) for g in range(1, groups)]
    scales = [weights] + [send(weights, same, g) for g in range(1, groups)]
    near, ids, scales = lax.optimization_barrier((jnp.concatenate(table), ids, scales))
    far = send(near, same, 0, 1) if cores > 1 else near

    sizes = (slabs, groups, cores, pieces, groups, nb, bs)
    smem = pl.BlockSpec(memory_space=pltpu.SMEM)
    vmem = pl.BlockSpec(memory_space=pltpu.VMEM)
    f32, bf16 = jnp.float32, jnp.bfloat16
    square = lambda dtype: pltpu.VMEM((order, order), dtype)
    slots = 3 * pieces
    kept, sent = pl.pallas_call(
        functools.partial(step_kernel, sizes),
        out_shape=(
            jax.ShapeDtypeStruct((2, slots, bs, bs), f32),
            jax.ShapeDtypeStruct((2, slots, bs, bs), bf16),
        ),
        in_specs=[smem] * (2 * groups + 1) + [vmem, vmem],
        out_specs=(vmem, vmem),
        scratch_shapes=[
            square(bf16),
            pltpu.VMEM((order // wide, wide, wide), bf16),
            pltpu.VMEM((nb, bs, bs), bf16),
            pltpu.VMEM((nb, bs, bs), bf16),
            square(bf16), square(bf16), square(bf16), square(bf16),
            square(f32), square(f32),
        ] * groups,
        compiler_params=pltpu.CompilerParams(vmem_limit_bytes=24 * 2**20),
        name="submatrix_step",
    )(*ids, *scales, potential, near, far)
    kept = [kept[:, i * pieces : (i + 1) * pieces] for i in range(3)]
    if cores > 1:
        other = send(sent, same, 0, 1)
        kept = [
            part + other[:, i * pieces : (i + 1) * pieces].astype(f32) for i, part in enumerate(kept)
        ]
    below = send(kept[0].astype(bf16), lambda s: s - 1)
    above = send(kept[2].astype(bf16), lambda s: s + 1)
    return tuple(kept[1][i] + below[i].astype(f32) + above[i].astype(f32) for i in range(2))


def solution(mesh):
    placed = (P(AXES, None, None), P(AXES, None), P(AXES, None), P())

    return jax.shard_map(
        shards,
        mesh=mesh,
        in_specs=placed,
        out_specs=(P(AXES, None, None), P(AXES, None, None)),
        check_vma=False,
    )
```

profile of v0, /device:TPU:0, one launch (start us, length us, event | category | flops | bytes accessed | tf_op | source)
XLA Modules:
  0.0 47.1 jit_solution(7073429296607368308)
XLA Ops:
  0.6 0.0 copy-start
  0.6 0.0 copy-start.1
  0.7 6.1 %collective-permute-start = (bf16[4,128,128]{2,1,0:T(8,128)(2,1)}, bf16[4,128,128]{2,1,0:T(8,128)(2,1)S(1)}, u32[]{:S(2)}, u32[]{:S(2)}) collective-permute-start(bf16[4,128,128]{2,1,0:T(8,128)(2,1)} %param.4), channel_id=1, source_target_pairs={{0,28},{1,29},{2,30},{3,31},{4,8},{5,9},{6,10},{7,11},{8,4},{9,5},... | collective-permute-start | bytes 393224 | tf_op jit(solution)/shard_map/ppermute | solution.py:198
  6.7 1.5 %collective-permute-start.3 = (bf16[4,128,128]{2,1,0:T(8,128)(2,1)}, bf16[4,128,128]{2,1,0:T(8,128)(2,1)S(1)}, u32[]{:S(2)}, u32[]{:S(2)}) collective-permute-start(bf16[4,128,128]{2,1,0:T(8,128)(2,1)} %param.4), channel_id=1, source_target_pairs={{0,2},{1,3},{2,0},{3,1},{4,6},{5,7},{6,4},{7,5},{8,10},{9,11},{10,... | collective-permute-start | bytes 393224 | tf_op jit(solution)/shard_map/ppermute | solution.py:198
  8.2 0.0 collective-permute-start.1
  8.2 2.0 %collective-permute-start.4 = (bf16[4,128,128]{2,1,0:T(8,128)(2,1)}, bf16[4,128,128]{2,1,0:T(8,128)(2,1)S(1)}, u32[]{:S(2)}, u32[]{:S(2)}) collective-permute-start(bf16[4,128,128]{2,1,0:T(8,128)(2,1)} %param.4), channel_id=1, source_target_pairs={{0,6},{1,7},{2,4},{3,5},{4,2},{5,3},{6,0},{7,1},{8,14},{9,15},{10,... | collective-permute-start | bytes 393224 | tf_op jit(solution)/shard_map/ppermute | solution.py:198
  10.2 1.5 %collective-permute-start.5 = (s32[1,10]{1,0:T(1,128)}, s32[1,10]{1,0:T(1,128)S(1)}, u32[]{:S(2)}, u32[]{:S(2)}) collective-permute-start(s32[1,10]{1,0:T(1,128)} %refs_0_), channel_id=1, source_target_pairs={{0,2},{1,3},{2,0},{3,1},{4,6},{5,7},{6,4},{7,5},{8,10},{9,11},{10,... | collective-permute-start | bytes 128 | tf_op jit(solution)/shard_map/ppermute | solution.py:198
  11.7 0.0 collective-permute-done
  11.7 0.5 %collective-permute-start.2 = (bf16[4,128,128]{2,1,0:T(8,128)(2,1)S(1)}, bf16[4,128,128]{2,1,0:T(8,128)(2,1)S(1)}, u32[]{:S(2)}, u32[]{:S(2)}) collective-permute-start(bf16[4,128,128]{2,1,0:T(8,128)(2,1)S(1)} %collective-permute-done), channel_id=1, source_target_pairs={{0,2},{1,3},{2,0},{3,1},{4,6},{5,7},{6,4},{7,5},{8,10},{9,11},{10,... | collective-permute-start | bytes 393224 | tf_op jit(solution)/shard_map/ppermute | solution.py:198
  12.3 0.9 %constant_dynamic-update-slice_fusion.4 = bf16[24,128,128]{2,1,0:T(8,128)(2,1)S(1)} fusion(bf16[24,128,128]{2,1,0:T(8,128)(2,1)S(1)} %constant_dynamic-update-slice_fusion.5, bf16[4,128,128]{2,1,0:T(8,128)(2,1)} %param.4), kind=kLoop, calls=%fused_computation.13 | loop fusion | bytes 262144
  13.2 2.9 %collective-permute-done.1 = bf16[4,128,128]{2,1,0:T(8,128)(2,1)S(1)} collective-permute-done((bf16[4,128,128]{2,1,0:T(8,128)(2,1)}, bf16[4,128,128]{2,1,0:T(8,128)(2,1)S(1)}, u32[]{:S(2)}, u32[]{:S(2)}) %collective-permute-start.1) | collective-permute-done | bytes 131104 | tf_op jit(solution)/shard_map/ppermute | solution.py:198
  16.1 1.5 %collective-permute-start.6 = (f32[1,10]{1,0:T(1,128)}, f32[1,10]{1,0:T(1,128)S(1)}, u32[]{:S(2)}, u32[]{:S(2)}) collective-permute-start(f32[1,10]{1,0:T(1,128)} %refs_2_), channel_id=1, source_target_pairs={{0,2},{1,3},{2,0},{3,1},{4,6},{5,7},{6,4},{7,5},{8,10},{9,11},{10,... | collective-permute-start | bytes 128 | tf_op jit(solution)/shard_map/ppermute | solution.py:198
  17.6 0.0 collective-permute-done.2
  17.6 0.0 collective-permute-done.3
  17.7 0.0 collective-permute-done.4
  17.7 0.0 collective-permute-done.5.refs_1_
  17.7 2.1 %collective-permute-done.6.refs_3_ = f32[1,10]{1,0:T(1,128)S(1)} collective-permute-done((f32[1,10]{1,0:T(1,128)}, f32[1,10]{1,0:T(1,128)S(1)}, u32[]{:S(2)}, u32[]{:S(2)}) %collective-permute-start.6) | collective-permute-done | bytes 72 | tf_op jit(solution)/shard_map/ppermute | solution.py:198
  19.8 0.0 collective-permute-start.7
  20.4 1.6 %collective-permute-done.7.refs_6_ = bf16[24,128,128]{2,1,0:T(8,128)(2,1)S(1)} collective-permute-done((bf16[24,128,128]{2,1,0:T(8,128)(2,1)S(1)}, bf16[24,128,128]{2,1,0:T(8,128)(2,1)S(1)}, u32[]{:S(2)}, u32[]{:S(2)}) %collective-permute-start.7) | collective-permute-done | bytes 786464 | tf_op jit(solution)/shard_map/ppermute | solution.py:198
  22.1 0.0 copy-done
  22.1 0.0 copy-done.1
  22.1 7.6 %submatrix_step.1 = (f32[2,12,128,128]{3,2,1,0:T(8,128)S(1)}, bf16[2,12,128,128]{3,2,1,0:T(8,128)(2,1)S(1)}) custom-call(s32[1,10]{1,0:T(1,128)S(1)} %copy-done, s32[1,10]{1,0:T(1,128)S(1)} %collective-permute-done.5.refs_1_, f32[1,10]{1,0:T(1,128)S(1)} %copy-done.1, f32[1,10]{1,0:T(1,128)S(1)} %collective-permute-done.6.refs_3_, f32[1]{0:T(128)S(6)} %copy.11.refs_4_, ...), custom_call_target="tpu_custom_call" | custom-call | tf_op jit(solution)/shard_map/submatrix_step/pallas_call | solution.py:219
  29.7 0.2 collective-permute-start.8
  29.8 2.2 %collective-permute-done.8 = bf16[2,12,128,128]{3,2,1,0:T(8,128)(2,1)S(1)} collective-permute-done((bf16[2,12,128,128]{3,2,1,0:T(8,128)(2,1)S(1)}, bf16[2,12,128,128]{3,2,1,0:T(8,128)(2,1)S(1)}, u32[]{:S(2)}, u32[]{:S(2)}) %collective-permute-start.8) | collective-permute-done | bytes 786464 | tf_op jit(solution)/shard_map/ppermute | solution.py:198
  32.0 0.2 add_convert_fusion.1
  32.2 3.2 %collective-permute-start.9 = (bf16[2,4,128,128]{3,2,1,0:T(8,128)(2,1)S(1)}, bf16[2,4,128,128]{3,2,1,0:T(8,128)(2,1)S(1)}, u32[]{:S(2)}, u32[]{:S(2)}) collective-permute-start(bf16[2,4,128,128]{3,2,1,0:T(8,128)(2,1)S(1)} %get-tuple-element.16), channel_id=1, source_target_pairs={{0,28},{1,29},{2,30},{3,31},{4,0},{5,1},{6,2},{7,3},{8,4},{9,5},{1... | collective-permute-start | bytes 786440 | tf_op jit(solution)/shard_map/ppermute | solution.py:198
  35.4 0.0 collective-permute-start.10
  35.4 5.9 %collective-permute-done.9 = bf16[2,4,128,128]{3,2,1,0:T(8,128)(2,1)S(1)} collective-permute-done((bf16[2,4,128,128]{3,2,1,0:T(8,128)(2,1)S(1)}, bf16[2,4,128,128]{3,2,1,0:T(8,128)(2,1)S(1)}, u32[]{:S(2)}, u32[]{:S(2)}) %collective-permute-start.9) | collective-permute-done | bytes 262176 | tf_op jit(solution)/shard_map/ppermute | solution.py:198
  41.2 5.0 %collective-permute-done.10 = bf16[2,4,128,128]{3,2,1,0:T(8,128)(2,1)S(1)} collective-permute-done((bf16[2,4,128,128]{3,2,1,0:T(8,128)(2,1)S(1)}, bf16[2,4,128,128]{3,2,1,0:T(8,128)(2,1)S(1)}, u32[]{:S(2)}, u32[]{:S(2)}) %collective-permute-start.10) | collective-permute-done | bytes 262176 | tf_op jit(solution)/shard_map/ppermute | solution.py:198
  46.2 0.9 %fusion.1 = (f32[4,128,128]{2,1,0:T(8,128)}, f32[4,128,128]{2,1,0:T(8,128)}) fusion(f32[2,4,128,128]{3,2,1,0:T(8,128)S(1)} %get-tuple-element.18, bf16[2,4,128,128]{3,2,1,0:T(8,128)(2,1)S(1)} %collective-permute-done.10, bf16[2,4,128,128]{3,2,1,0:T(8,128)(2,1)S(1)} %collective-permute-done.9), kind=kLoop, calls=%fused_computation.5 | loop fusion | flops 524288 | bytes 1572864 | tf_op jit(solution)/shard_map/add | solution.py:246
  (5 shorter events, 0.1 us)
Async XLA Ops:
  0.6 21.4 %copy-start = (s32[1,10]{1,0:T(1,128)S(1)}, s32[1,10]{1,0:T(1,128)}, u32[]{:S(2)}) copy-start(s32[1,10]{1,0:T(1,128)} %refs_0_) | copy-start | bytes 124
  0.6 21.4 %copy-start.1 = (f32[1,10]{1,0:T(1,128)S(1)}, f32[1,10]{1,0:T(1,128)}, u32[]{:S(2)}) copy-start(f32[1,10]{1,0:T(1,128)} %refs_2_) | copy-start | bytes 124
  0.7 11.1 %collective-permute-start = (bf16[4,128,128]{2,1,0:T(8,128)(2,1)}, bf16[4,128,128]{2,1,0:T(8,128)(2,1)S(1)}, u32[]{:S(2)}, u32[]{:S(2)}) collective-permute-start(bf16[4,128,128]{2,1,0:T(8,128)(2,1)} %param.4), channel_id=1, source_target_pairs={{0,28},{1,29},{2,30},{3,31},{4,8},{5,9},{6,10},{7,11},{8,4},{9,5},... | collective-permute-start | bytes 393224 | tf_op jit(solution)/shard_map/ppermute | solution.py:198
  6.7 10.9 %collective-permute-start.3 = (bf16[4,128,128]{2,1,0:T(8,128)(2,1)}, bf16[4,128,128]{2,1,0:T(8,128)(2,1)S(1)}, u32[]{:S(2)}, u32[]{:S(2)}) collective-permute-start(bf16[4,128,128]{2,1,0:T(8,128)(2,1)} %param.4), channel_id=1, source_target_pairs={{0,2},{1,3},{2,0},{3,1},{4,6},{5,7},{6,4},{7,5},{8,10},{9,11},{10,... | collective-permute-start | bytes 393224 | tf_op jit(solution)/shard_map/ppermute | solution.py:198
  8.2 7.8 %collective-permute-start.1 = (bf16[4,128,128]{2,1,0:T(8,128)(2,1)}, bf16[4,128,128]{2,1,0:T(8,128)(2,1)S(1)}, u32[]{:S(2)}, u32[]{:S(2)}) collective-permute-start(bf16[4,128,128]{2,1,0:T(8,128)(2,1)} %param.4), channel_id=1, source_target_pairs={{0,4},{1,5},{2,6},{3,7},{4,0},{5,1},{6,2},{7,3},{8,12},{9,13},{10,... | collective-permute-start | bytes 393224 | tf_op jit(solution)/shard_map/ppermute | solution.py:198
  8.2 9.4 %collective-permute-start.4 = (bf16[4,128,128]{2,1,0:T(8,128)(2,1)}, bf16[4,128,128]{2,1,0:T(8,128)(2,1)S(1)}, u32[]{:S(2)}, u32[]{:S(2)}) collective-permute-start(bf16[4,128,128]{2,1,0:T(8,128)(2,1)} %param.4), channel_id=1, source_target_pairs={{0,6},{1,7},{2,4},{3,5},{4,2},{5,3},{6,0},{7,1},{8,14},{9,15},{10,... | collective-permute-start | bytes 393224 | tf_op jit(solution)/shard_map/ppermute | solution.py:198
  10.2 7.5 %collective-permute-start.5 = (s32[1,10]{1,0:T(1,128)}, s32[1,10]{1,0:T(1,128)S(1)}, u32[]{:S(2)}, u32[]{:S(2)}) collective-permute-start(s32[1,10]{1,0:T(1,128)} %refs_0_), channel_id=1, source_target_pairs={{0,2},{1,3},{2,0},{3,1},{4,6},{5,7},{6,4},{7,5},{8,10},{9,11},{10,... | collective-permute-start | bytes 128 | tf_op jit(solution)/shard_map/ppermute | solution.py:198
  11.7 5.9 %collective-permute-start.2 = (bf16[4,128,128]{2,1,0:T(8,128)(2,1)S(1)}, bf16[4,128,128]{2,1,0:T(8,128)(2,1)S(1)}, u32[]{:S(2)}, u32[]{:S(2)}) collective-permute-start(bf16[4,128,128]{2,1,0:T(8,128)(2,1)S(1)} %collective-permute-done), channel_id=1, source_target_pairs={{0,2},{1,3},{2,0},{3,1},{4,6},{5,7},{6,4},{7,5},{8,10},{9,11},{10,... | collective-permute-start | bytes 393224 | tf_op jit(solution)/shard_map/ppermute | solution.py:198
  16.1 3.7 %collective-permute-start.6 = (f32[1,10]{1,0:T(1,128)}, f32[1,10]{1,0:T(1,128)S(1)}, u32[]{:S(2)}, u32[]{:S(2)}) collective-permute-start(f32[1,10]{1,0:T(1,128)} %refs_2_), channel_id=1, source_target_pairs={{0,2},{1,3},{2,0},{3,1},{4,6},{5,7},{6,4},{7,5},{8,10},{9,11},{10,... | collective-permute-start | bytes 128 | tf_op jit(solution)/shard_map/ppermute | solution.py:198
  19.8 2.3 %collective-permute-start.7 = (bf16[24,128,128]{2,1,0:T(8,128)(2,1)S(1)}, bf16[24,128,128]{2,1,0:T(8,128)(2,1)S(1)}, u32[]{:S(2)}, u32[]{:S(2)}) collective-permute-start(bf16[24,128,128]{2,1,0:T(8,128)(2,1)S(1)} %constant_dynamic-update-slice_fusion.refs_5_), channel_id=1, source_target_pairs={{0,1},{1,0},{2,3},{3,2},{4,5},{5,4},{6,7},{7,6},{8,9},{9,8},{10,11... | collective-permute-start | bytes 2359304 | tf_op jit(solution)/shard_map/ppermute | solution.py:198
  29.7 2.4 %collective-permute-start.8 = (bf16[2,12,128,128]{3,2,1,0:T(8,128)(2,1)S(1)}, bf16[2,12,128,128]{3,2,1,0:T(8,128)(2,1)S(1)}, u32[]{:S(2)}, u32[]{:S(2)}) collective-permute-start(bf16[2,12,128,128]{3,2,1,0:T(8,128)(2,1)S(1)} %get-tuple-element.15), channel_id=1, source_target_pairs={{0,1},{1,0},{2,3},{3,2},{4,5},{5,4},{6,7},{7,6},{8,9},{9,8},{10,11... | collective-permute-start | bytes 2359304 | tf_op jit(solution)/shard_map/ppermute | solution.py:198
  32.2 9.0 %collective-permute-start.9 = (bf16[2,4,128,128]{3,2,1,0:T(8,128)(2,1)S(1)}, bf16[2,4,128,128]{3,2,1,0:T(8,128)(2,1)S(1)}, u32[]{:S(2)}, u32[]{:S(2)}) collective-permute-start(bf16[2,4,128,128]{3,2,1,0:T(8,128)(2,1)S(1)} %get-tuple-element.16), channel_id=1, source_target_pairs={{0,28},{1,29},{2,30},{3,31},{4,0},{5,1},{6,2},{7,3},{8,4},{9,5},{1... | collective-permute-start | bytes 786440 | tf_op jit(solution)/shard_map/ppermute | solution.py:198
  35.4 10.9 %collective-permute-start.10 = (bf16[2,4,128,128]{3,2,1,0:T(8,128)(2,1)S(1)}, bf16[2,4,128,128]{3,2,1,0:T(8,128)(2,1)S(1)}, u32[]{:S(2)}, u32[]{:S(2)}) collective-permute-start(bf16[2,4,128,128]{3,2,1,0:T(8,128)(2,1)S(1)} %get-tuple-element.17), channel_id=1, source_target_pairs={{0,4},{1,5},{2,6},{3,7},{4,8},{5,9},{6,10},{7,11},{8,12},{9,13},{1... | collective-permute-start | bytes 786440 | tf_op jit(solution)/shard_map/ppermute | solution.py:198
where the time goes:
time: 47.3 us; the launch traced here: 47.1 us
  waiting for transfers between devices  19.6 us (41%)
  starting transfers between devices  16.4 us (35%)
  Pallas kernels  7.57 us (16%)
  between operations  1.39 us (3%)
  other arithmetic  1.09 us (2%)
  local copies, waits for them, and re-layouts  1.02 us (2%)
    ppermute x11, waiting for transfers between devices, send(): return lax.ppermute(value, AXES, pairs)  19.6 us
    ppermute x11, starting transfers between devices, send(): return lax.ppermute(value, AXES, pairs)  16.4 us
    pallas_call x1, Pallas kernels, shards(): pl.pallas_call(functools.partial(step_kernel, sizes), out_shape=(jax.Shap...  7.57 us
    unnamed x9, local copies, waits for them, and re-layouts  1 us
  transfers between devices with their start and end apart: 11, of which 6 were waited for; matrix products, arithmetic and copies ran while one was open for 2% of the time, Pallas kernels for 0%

commit v1 on v0

--- a/solution.py
+++ b/solution.py
@@ -30,8 +30,9 @@
 def step_kernel(sizes, *refs):
     slabs, groups, cores, pieces, rows, nb, bs = sizes
     ids, weights = refs[:rows], refs[rows : 2 * rows]
-    potential, near, far, kept, sent = refs[2 * rows : 2 * rows + 5]
-    scratch = refs[2 * rows + 5 :]
+    potential, refs = refs[2 * rows], refs[2 * rows + 1 :]
+    sources, refs = refs[: 2 * cores], refs[2 * cores :]
+    kept, sent, table, scratch = refs[0], refs[1], refs[2], refs[3:]
     per_row = len(scratch) // rows
     order = nb * bs
     wide = min(2 * bs, order)
@@ -78,6 +79,12 @@
         part = index * bs % wide
         return index * bs // wide, pl.ds(part, bs), pl.ds(part, bs)
 
+    at = 0
+    for source in sources:
+        count = source.shape[0]
+        table[pl.ds(at, count)] = source[...]
+        at += count
+
     spots = [[where_is(row, k) for k in range(len(pairs))] for row in range(rows)]
     state = [scratch[row * per_row : (row + 1) * per_row] for row in range(rows)]
     inverses = []
@@ -90,10 +97,17 @@
             offset, group, core, slot = spots[row][k]
             turn = (here_group - group + groups) % groups
             place = jnp.where(here_slab % 2 == 0, offset, 2 - offset)
-            index = (turn * 3 + place) * pieces + slot
-            block = near[index]
-            if cores > 1:
-                block = jnp.where(core == here_core, block, far[index])
+            piece = jnp.where(
+                place == 1,
+                jnp.where(turn == 0, 0, 1 + turn),
+                jnp.where(
+                    place == 2,
+                    jnp.where(turn == 0, 1, groups + 1 + turn),
+                    jnp.where(turn == 0, groups + 1, 2 * groups + turn),
+                ),
+            )
+            piece += jnp.where(core == here_core, 0, 3 * groups)
+            block = table[piece * pieces + slot]
             wide_block = block.astype(f32)
             if a == b:
                 ham = wide_block + wide_block.T
@@ -200,15 +214,21 @@
     same = lambda s: s
     first = lambda s: s - 1 if s % 2 else s + 1
     second = lambda s: s + 1 if s % 2 else s - 1
-    table = [send(hamilton_blocks, second), hamilton_blocks, send(hamilton_blocks, first)]
-    for g in range(1, groups):
-        table += [
-            send(table[0], same, g), send(hamilton_blocks, same, g), send(hamilton_blocks, first, g)
-        ]
+    far_slab = send(hamilton_blocks, second)
+    near = [hamilton_blocks, send(hamilton_blocks, first)]
+    near += [send(hamilton_blocks, same, g) for g in range(1, groups)]
+    late = [far_slab]
+    late += [send(hamilton_blocks, first, g) for g in range(1, groups)]
+    late += [send(far_slab, same, g) for g in range(1, groups)]
+    near.append(jnp.concatenate(late))
     ids = [pair_ids] + [send(pair_ids, same, g) for g in range(1, groups)]
     scales = [weights] + [send(weights, same, g) for g in range(1, groups)]
-    near, ids, scales = lax.optimization_barrier((jnp.concatenate(table), ids, scales))
-    far = send(near, same, 0, 1) if cores > 1 else near
+    near = [jnp.concatenate(near[:-1]), near[-1]]
+    blocks = near
+    if cores > 1:
+        early = send(near[0], same, 0, 1)
+        near, ids, scales = lax.optimization_barrier((near, ids, scales))
+        blocks = near + [early, send(near[1], same, 0, 1)]
 
     sizes = (slabs, groups, cores, pieces, groups, nb, bs)
     smem = pl.BlockSpec(memory_space=pltpu.SMEM)
@@ -222,9 +242,10 @@
             jax.ShapeDtypeStruct((2, slots, bs, bs), f32),
             jax.ShapeDtypeStruct((2, slots, bs, bs), bf16),
         ),
-        in_specs=[smem] * (2 * groups + 1) + [vmem, vmem],
+        in_specs=[smem] * (2 * groups + 1) + [vmem] * len(blocks),
         out_specs=(vmem, vmem),
-        scratch_shapes=[
+        scratch_shapes=[pltpu.VMEM((cores * 3 * groups * pieces, bs, bs), bf16)]
+        + [
             square(bf16),
             pltpu.VMEM((order // wide, wide, wide), bf16),
             pltpu.VMEM((nb, bs, bs), bf16),
@@ -234,7 +255,7 @@
         ] * groups,
         compiler_params=pltpu.CompilerParams(vmem_limit_bytes=24 * 2**20),
         name="submatrix_step",
-    )(*ids, *scales, potential, near, far)
+    )(*ids, *scales, potential, *blocks)
     kept = [kept[:, i * pieces : (i + 1) * pieces] for i in range(3)]
     if cores > 1:
         other = send(sent, same, 0, 1)

time: 47.3 us -> 48.2 us (1.019)
  starting transfers between devices: 16.4 us -> 18.9 us
  waiting for transfers between devices: 19.6 us -> 18 us
    ppermute x11 -> x12, starting transfers between devices: 16.4 us -> 18.9 us  [send(): return lax.ppermute(value, AXES, pairs)]
    ppermute x11 -> x12, waiting for transfers between devices: 19.6 us -> 18 us  [send(): return lax.ppermute(value, AXES, pairs)]
    unnamed x9 -> x6, local copies, waits for them, and re-layouts: 1 us -> 0.94 us
  transfers between devices with their start and end apart: 11 -> 12, of which waited for: 6 -> 7; matrix products, arithmetic and copies ran while one was open for 2% -> 2% of each run, Pallas kernels for 0% -> 0%
where the time goes in v1:
time: 48.2 us; the launch traced here: 48 us
  starting transfers between devices  18.9 us (39%)
  waiting for transfers between devices  18 us (37%)
  Pallas kernels  7.62 us (16%)
  between operations  1.38 us (3%)
  other arithmetic  1.13 us (2%)
  local copies, waits for them, and re-layouts  0.96 us (2%)
    ppermute x12, starting transfers between devices, send(): return lax.ppermute(value, AXES, pairs)  18.9 us
    ppermute x12, waiting for transfers between devices, send(): return lax.ppermute(value, AXES, pairs)  18 us
    pallas_call x1, Pallas kernels, shards(): pl.pallas_call(functools.partial(step_kernel, sizes), out_shape=(jax.Shap...  7.62 us
  transfers between devices with their start and end apart: 12, of which 7 were waited for; matrix products, arithmetic and copies ran while one was open for 2% of the time, Pallas kernels for 0%

profile of v1, /device:TPU:0, one launch (start us, length us, event | category | flops | bytes accessed | tf_op | source)
XLA Modules:
  0.0 48.0 jit_solution(16414756443257319673)
XLA Ops:
  0.6 0.0 copy-start
  0.6 0.0 copy-start.1
  0.7 3.1 %collective-permute-start = (bf16[4,128,128]{2,1,0:T(8,128)(2,1)}, bf16[4,128,128]{2,1,0:T(8,128)(2,1)S(1)}, u32[]{:S(2)}, u32[]{:S(2)}) collective-permute-start(bf16[4,128,128]{2,1,0:T(8,128)(2,1)} %param.4), channel_id=1, source_target_pairs={{0,4},{1,5},{2,6},{3,7},{4,0},{5,1},{6,2},{7,3},{8,12},{9,13},{10,... | collective-permute-start | bytes 393224 | tf_op jit(solution)/shard_map/ppermute | solution.py:212
  3.7 3.5 %collective-permute-start.2 = (bf16[4,128,128]{2,1,0:T(8,128)(2,1)}, bf16[4,128,128]{2,1,0:T(8,128)(2,1)S(1)}, u32[]{:S(2)}, u32[]{:S(2)}) collective-permute-start(bf16[4,128,128]{2,1,0:T(8,128)(2,1)} %param.4), channel_id=1, source_target_pairs={{0,28},{1,29},{2,30},{3,31},{4,8},{5,9},{6,10},{7,11},{8,4},{9,5},... | collective-permute-start | bytes 393224 | tf_op jit(solution)/shard_map/ppermute | solution.py:212
  7.3 1.5 %collective-permute-start.1 = (bf16[4,128,128]{2,1,0:T(8,128)(2,1)}, bf16[4,128,128]{2,1,0:T(8,128)(2,1)S(1)}, u32[]{:S(2)}, u32[]{:S(2)}) collective-permute-start(bf16[4,128,128]{2,1,0:T(8,128)(2,1)} %param.4), channel_id=1, source_target_pairs={{0,2},{1,3},{2,0},{3,1},{4,6},{5,7},{6,4},{7,5},{8,10},{9,11},{10,... | collective-permute-start | bytes 393224 | tf_op jit(solution)/shard_map/ppermute | solution.py:212
  8.7 0.0 collective-permute-start.3
  8.8 1.0 %collective-permute-start.5 = (s32[1,10]{1,0:T(1,128)}, s32[1,10]{1,0:T(1,128)S(1)}, u32[]{:S(2)}, u32[]{:S(2)}) collective-permute-start(s32[1,10]{1,0:T(1,128)} %refs_0_), channel_id=1, source_target_pairs={{0,2},{1,3},{2,0},{3,1},{4,6},{5,7},{6,4},{7,5},{8,10},{9,11},{10,... | collective-permute-start | bytes 128 | tf_op jit(solution)/shard_map/ppermute | solution.py:212
  9.7 0.9 %constant_dynamic-update-slice_fusion.2 = bf16[12,128,128]{2,1,0:T(8,128)(2,1)S(1)} fusion(bf16[4,128,128]{2,1,0:T(8,128)(2,1)} %param.4), kind=kLoop, calls=%fused_computation.12 | loop fusion | bytes 262144
  10.6 0.0 collective-permute-done
  10.6 1.1 %collective-permute-start.6 = (f32[1,10]{1,0:T(1,128)}, f32[1,10]{1,0:T(1,128)S(1)}, u32[]{:S(2)}, u32[]{:S(2)}) collective-permute-start(f32[1,10]{1,0:T(1,128)} %refs_2_), channel_id=1, source_target_pairs={{0,2},{1,3},{2,0},{3,1},{4,6},{5,7},{6,4},{7,5},{8,10},{9,11},{10,... | collective-permute-start | bytes 128 | tf_op jit(solution)/shard_map/ppermute | solution.py:212
  11.8 0.0 collective-permute-done.2
  11.8 1.9 %collective-permute-start.4 = (bf16[4,128,128]{2,1,0:T(8,128)(2,1)S(1)}, bf16[4,128,128]{2,1,0:T(8,128)(2,1)S(1)}, u32[]{:S(2)}, u32[]{:S(2)}) collective-permute-start(bf16[4,128,128]{2,1,0:T(8,128)(2,1)S(1)} %collective-permute-done.2), channel_id=1, source_target_pairs={{0,2},{1,3},{2,0},{3,1},{4,6},{5,7},{6,4},{7,5},{8,10},{9,11},{10,... | collective-permute-start | bytes 393224 | tf_op jit(solution)/shard_map/ppermute | solution.py:212
  13.6 0.2 collective-permute-done.1
  13.9 0.1 collective-permute-start.7
  13.9 1.5 %collective-permute-done.3 = bf16[4,128,128]{2,1,0:T(8,128)(2,1)S(1)} collective-permute-done((bf16[4,128,128]{2,1,0:T(8,128)(2,1)}, bf16[4,128,128]{2,1,0:T(8,128)(2,1)S(1)}, u32[]{:S(2)}, u32[]{:S(2)}) %collective-permute-start.3) | collective-permute-done | bytes 131104 | tf_op jit(solution)/shard_map/ppermute | solution.py:212
  15.5 2.3 %collective-permute-done.4 = bf16[4,128,128]{2,1,0:T(8,128)(2,1)S(1)} collective-permute-done((bf16[4,128,128]{2,1,0:T(8,128)(2,1)S(1)}, bf16[4,128,128]{2,1,0:T(8,128)(2,1)S(1)}, u32[]{:S(2)}, u32[]{:S(2)}) %collective-permute-start.4) | collective-permute-done | bytes 131104 | tf_op jit(solution)/shard_map/ppermute | solution.py:212
  17.8 0.0 collective-permute-done.5.refs_1_
  17.8 0.0 collective-permute-done.6.refs_3_
  17.9 0.1 collective-permute-start.8
  18.6 0.0 collective-permute-done.7.refs_7_
  18.6 1.1 %collective-permute-done.8.refs_8_ = bf16[12,128,128]{2,1,0:T(8,128)(2,1)S(1)} collective-permute-done((bf16[12,128,128]{2,1,0:T(8,128)(2,1)S(1)}, bf16[12,128,128]{2,1,0:T(8,128)(2,1)S(1)}, u32[]{:S(2)}, u32[]{:S(2)}) %collective-permute-start.8) | collective-permute-done | bytes 393248 | tf_op jit(solution)/shard_map/ppermute | solution.py:212
  19.6 0.0 copy-done
  19.6 0.0 copy-done.1
  19.6 7.6 %submatrix_step.1 = (f32[2,12,128,128]{3,2,1,0:T(8,128)S(1)}, bf16[2,12,128,128]{3,2,1,0:T(8,128)(2,1)S(1)}) custom-call(s32[1,10]{1,0:T(1,128)S(1)} %copy-done, s32[1,10]{1,0:T(1,128)S(1)} %collective-permute-done.5.refs_1_, f32[1,10]{1,0:T(1,128)S(1)} %copy-done.1, f32[1,10]{1,0:T(1,128)S(1)} %collective-permute-done.6.refs_3_, f32[1]{0:T(128)S(6)} %copy.8.refs_4_, ...), custom_call_target="tpu_custom_call" | custom-call | tf_op jit(solution)/shard_map/submatrix_step/pallas_call | solution.py:239
  27.3 0.2 collective-permute-start.9
  27.4 2.2 %collective-permute-done.9 = bf16[2,12,128,128]{3,2,1,0:T(8,128)(2,1)S(1)} collective-permute-done((bf16[2,12,128,128]{3,2,1,0:T(8,128)(2,1)S(1)}, bf16[2,12,128,128]{3,2,1,0:T(8,128)(2,1)S(1)}, u32[]{:S(2)}, u32[]{:S(2)}) %collective-permute-start.9) | collective-permute-done | bytes 786464 | tf_op jit(solution)/shard_map/ppermute | solution.py:212
  29.6 0.2 add_convert_fusion.1
  29.8 6.5 %collective-permute-start.10 = (bf16[2,4,128,128]{3,2,1,0:T(8,128)(2,1)S(1)}, bf16[2,4,128,128]{3,2,1,0:T(8,128)(2,1)S(1)}, u32[]{:S(2)}, u32[]{:S(2)}) collective-permute-start(bf16[2,4,128,128]{3,2,1,0:T(8,128)(2,1)S(1)} %get-tuple-element.18), channel_id=1, source_target_pairs={{0,28},{1,29},{2,30},{3,31},{4,0},{5,1},{6,2},{7,3},{8,4},{9,5},{1... | collective-permute-start | bytes 786440 | tf_op jit(solution)/shard_map/ppermute | solution.py:212
  36.4 0.0 collective-permute-start.11
  36.4 5.9 %collective-permute-done.10 = bf16[2,4,128,128]{3,2,1,0:T(8,128)(2,1)S(1)} collective-permute-done((bf16[2,4,128,128]{3,2,1,0:T(8,128)(2,1)S(1)}, bf16[2,4,128,128]{3,2,1,0:T(8,128)(2,1)S(1)}, u32[]{:S(2)}, u32[]{:S(2)}) %collective-permute-start.10) | collective-permute-done | bytes 262176 | tf_op jit(solution)/shard_map/ppermute | solution.py:212
  42.2 4.9 %collective-permute-done.11 = bf16[2,4,128,128]{3,2,1,0:T(8,128)(2,1)S(1)} collective-permute-done((bf16[2,4,128,128]{3,2,1,0:T(8,128)(2,1)S(1)}, bf16[2,4,128,128]{3,2,1,0:T(8,128)(2,1)S(1)}, u32[]{:S(2)}, u32[]{:S(2)}) %collective-permute-start.11) | collective-permute-done | bytes 262176 | tf_op jit(solution)/shard_map/ppermute | solution.py:212
  47.1 0.9 %fusion.1 = (f32[4,128,128]{2,1,0:T(8,128)}, f32[4,128,128]{2,1,0:T(8,128)}) fusion(f32[2,4,128,128]{3,2,1,0:T(8,128)S(1)} %get-tuple-element.20, bf16[2,4,128,128]{3,2,1,0:T(8,128)(2,1)S(1)} %collective-permute-done.11, bf16[2,4,128,128]{3,2,1,0:T(8,128)(2,1)S(1)} %collective-permute-done.10), kind=kLoop, calls=%fused_computation.6 | loop fusion | flops 524288 | bytes 1572864 | tf_op jit(solution)/shard_map/add | solution.py:267
  (3 shorter events, 0.1 us)
Async XLA Ops:
  0.6 19.0 %copy-start = (s32[1,10]{1,0:T(1,128)S(1)}, s32[1,10]{1,0:T(1,128)}, u32[]{:S(2)}) copy-start(s32[1,10]{1,0:T(1,128)} %refs_0_) | copy-start | bytes 124
  0.6 19.0 %copy-start.1 = (f32[1,10]{1,0:T(1,128)S(1)}, f32[1,10]{1,0:T(1,128)}, u32[]{:S(2)}) copy-start(f32[1,10]{1,0:T(1,128)} %refs_2_) | copy-start | bytes 124
  0.7 10.0 %collective-permute-start = (bf16[4,128,128]{2,1,0:T(8,128)(2,1)}, bf16[4,128,128]{2,1,0:T(8,128)(2,1)S(1)}, u32[]{:S(2)}, u32[]{:S(2)}) collective-permute-start(bf16[4,128,128]{2,1,0:T(8,128)(2,1)} %param.4), channel_id=1, source_target_pairs={{0,4},{1,5},{2,6},{3,7},{4,0},{5,1},{6,2},{7,3},{8,12},{9,13},{10,... | collective-permute-start | bytes 393224 | tf_op jit(solution)/shard_map/ppermute | solution.py:212
  3.7 8.1 %collective-permute-start.2 = (bf16[4,128,128]{2,1,0:T(8,128)(2,1)}, bf16[4,128,128]{2,1,0:T(8,128)(2,1)S(1)}, u32[]{:S(2)}, u32[]{:S(2)}) collective-permute-start(bf16[4,128,128]{2,1,0:T(8,128)(2,1)} %param.4), channel_id=1, source_target_pairs={{0,28},{1,29},{2,30},{3,31},{4,8},{5,9},{6,10},{7,11},{8,4},{9,5},... | collective-permute-start | bytes 393224 | tf_op jit(solution)/shard_map/ppermute | solution.py:212
  7.3 6.6 %collective-permute-start.1 = (bf16[4,128,128]{2,1,0:T(8,128)(2,1)}, bf16[4,128,128]{2,1,0:T(8,128)(2,1)S(1)}, u32[]{:S(2)}, u32[]{:S(2)}) collective-permute-start(bf16[4,128,128]{2,1,0:T(8,128)(2,1)} %param.4), channel_id=1, source_target_pairs={{0,2},{1,3},{2,0},{3,1},{4,6},{5,7},{6,4},{7,5},{8,10},{9,11},{10,... | collective-permute-start | bytes 393224 | tf_op jit(solution)/shard_map/ppermute | solution.py:212
  8.7 6.7 %collective-permute-start.3 = (bf16[4,128,128]{2,1,0:T(8,128)(2,1)}, bf16[4,128,128]{2,1,0:T(8,128)(2,1)S(1)}, u32[]{:S(2)}, u32[]{:S(2)}) collective-permute-start(bf16[4,128,128]{2,1,0:T(8,128)(2,1)} %param.4), channel_id=1, source_target_pairs={{0,6},{1,7},{2,4},{3,5},{4,2},{5,3},{6,0},{7,1},{8,14},{9,15},{10,... | collective-permute-start | bytes 393224 | tf_op jit(solution)/shard_map/ppermute | solution.py:212
  8.8 9.1 %collective-permute-start.5 = (s32[1,10]{1,0:T(1,128)}, s32[1,10]{1,0:T(1,128)S(1)}, u32[]{:S(2)}, u32[]{:S(2)}) collective-permute-start(s32[1,10]{1,0:T(1,128)} %refs_0_), channel_id=1, source_target_pairs={{0,2},{1,3},{2,0},{3,1},{4,6},{5,7},{6,4},{7,5},{8,10},{9,11},{10,... | collective-permute-start | bytes 128 | tf_op jit(solution)/shard_map/ppermute | solution.py:212
  10.6 7.2 %collective-permute-start.6 = (f32[1,10]{1,0:T(1,128)}, f32[1,10]{1,0:T(1,128)S(1)}, u32[]{:S(2)}, u32[]{:S(2)}) collective-permute-start(f32[1,10]{1,0:T(1,128)} %refs_2_), channel_id=1, source_target_pairs={{0,2},{1,3},{2,0},{3,1},{4,6},{5,7},{6,4},{7,5},{8,10},{9,11},{10,... | collective-permute-start | bytes 128 | tf_op jit(solution)/shard_map/ppermute | solution.py:212
  11.8 6.0 %collective-permute-start.4 = (bf16[4,128,128]{2,1,0:T(8,128)(2,1)S(1)}, bf16[4,128,128]{2,1,0:T(8,128)(2,1)S(1)}, u32[]{:S(2)}, u32[]{:S(2)}) collective-permute-start(bf16[4,128,128]{2,1,0:T(8,128)(2,1)S(1)} %collective-permute-done.2), channel_id=1, source_target_pairs={{0,2},{1,3},{2,0},{3,1},{4,6},{5,7},{6,4},{7,5},{8,10},{9,11},{10,... | collective-permute-start | bytes 393224 | tf_op jit(solution)/shard_map/ppermute | solution.py:212
  13.9 4.7 %collective-permute-start.7 = (bf16[12,128,128]{2,1,0:T(8,128)(2,1)S(1)}, bf16[12,128,128]{2,1,0:T(8,128)(2,1)S(1)}, u32[]{:S(2)}, u32[]{:S(2)}) collective-permute-start(bf16[12,128,128]{2,1,0:T(8,128)(2,1)S(1)} %constant_dynamic-update-slice_fusion.refs_5_), channel_id=1, source_target_pairs={{0,1},{1,0},{2,3},{3,2},{4,5},{5,4},{6,7},{7,6},{8,9},{9,8},{10,11... | collective-permute-start | bytes 1179656 | tf_op jit(solution)/shard_map/ppermute | solution.py:212
  17.9 1.8 %collective-permute-start.8 = (bf16[12,128,128]{2,1,0:T(8,128)(2,1)S(1)}, bf16[12,128,128]{2,1,0:T(8,128)(2,1)S(1)}, u32[]{:S(2)}, u32[]{:S(2)}) collective-permute-start(bf16[12,128,128]{2,1,0:T(8,128)(2,1)S(1)} %pad_maximum_fusion.refs_6_), channel_id=1, source_target_pairs={{0,1},{1,0},{2,3},{3,2},{4,5},{5,4},{6,7},{7,6},{8,9},{9,8},{10,11... | collective-permute-start | bytes 1179656 | tf_op jit(solution)/shard_map/ppermute | solution.py:212
  27.3 2.4 %collective-permute-start.9 = (bf16[2,12,128,128]{3,2,1,0:T(8,128)(2,1)S(1)}, bf16[2,12,128,128]{3,2,1,0:T(8,128)(2,1)S(1)}, u32[]{:S(2)}, u32[]{:S(2)}) collective-permute-start(bf16[2,12,128,128]{3,2,1,0:T(8,128)(2,1)S(1)} %get-tuple-element.17), channel_id=1, source_target_pairs={{0,1},{1,0},{2,3},{3,2},{4,5},{5,4},{6,7},{7,6},{8,9},{9,8},{10,11... | collective-permute-start | bytes 2359304 | tf_op jit(solution)/shard_map/ppermute | solution.py:212
  29.8 12.4 %collective-permute-start.10 = (bf16[2,4,128,128]{3,2,1,0:T(8,128)(2,1)S(1)}, bf16[2,4,128,128]{3,2,1,0:T(8,128)(2,1)S(1)}, u32[]{:S(2)}, u32[]{:S(2)}) collective-permute-start(bf16[2,4,128,128]{3,2,1,0:T(8,128)(2,1)S(1)} %get-tuple-element.18), channel_id=1, source_target_pairs={{0,28},{1,29},{2,30},{3,31},{4,0},{5,1},{6,2},{7,3},{8,4},{9,5},{1... | collective-permute-start | bytes 786440 | tf_op jit(solution)/shard_map/ppermute | solution.py:212
  36.4 10.8 %collective-permute-start.11 = (bf16[2,4,128,128]{3,2,1,0:T(8,128)(2,1)S(1)}, bf16[2,4,128,128]{3,2,1,0:T(8,128)(2,1)S(1)}, u32[]{:S(2)}, u32[]{:S(2)}) collective-permute-start(bf16[2,4,128,128]{3,2,1,0:T(8,128)(2,1)S(1)} %get-tuple-element.19), channel_id=1, source_target_pairs={{0,4},{1,5},{2,6},{3,7},{4,8},{5,9},{6,10},{7,11},{8,12},{9,13},{1... | collective-permute-start | bytes 786440 | tf_op jit(solution)/shard_map/ppermute | solution.py:212

commit v2 on v1

--- a/solution.py
+++ b/solution.py
@@ -31,7 +31,7 @@
     slabs, groups, cores, pieces, rows, nb, bs = sizes
     ids, weights = refs[:rows], refs[rows : 2 * rows]
     potential, refs = refs[2 * rows], refs[2 * rows + 1 :]
-    sources, refs = refs[: 2 * cores], refs[2 * cores :]
+    sources, refs = refs[: 3 * cores], refs[3 * cores :]
     kept, sent, table, scratch = refs[0], refs[1], refs[2], refs[3:]
     per_row = len(scratch) // rows
     order = nb * bs
@@ -160,6 +160,24 @@
         for i, row, upper, right in strips():
             _, _, _, _, a_hi, a_lo, _, _, full, _ = state[row]
             store_halves(a_hi, a_lo, upper, right, full[upper, right])
+
+    def parts(mat, row):
+        for k, (a, b) in enumerate(pairs):
+            offset, group, core, slot = spots[row][k]
+            part = weights[row][0, k] * state[row][8 + mat][cut(a), cut(b)]
+            same_group = group == here_group
+            mine = jnp.logical_and(same_group, core == here_core)
+            mates = jnp.logical_and(same_group, core != here_core)
+            yield offset * pieces + slot, mine, mates, part.astype(bf16).astype(f32)
+
+    def add(target, mat, at, part):
+        target[mat, at] = (target[mat, at].astype(f32) + part).astype(target.dtype)
+
+    for row in range(rows):
+        for at, mine, mates, part in parts(0, row):
+            add(kept, 0, at, jnp.where(mine, part, 0.0))
+            if cores > 1:
+                add(sent, 0, at, jnp.where(mates, part, 0.0))
     for i, row, upper, right in strips():
         base_hi, base_lo, _, _, a_hi, a_lo, _, _, _, full2 = state[row]
         value = mm(a_hi[upper, :], base_hi[:, right]) + mm(a_lo[upper, :], base_hi[:, right])
@@ -169,26 +187,10 @@
         )
         full2[upper, right] = value
     for row in range(rows):
-        full, full2 = state[row][8:]
-        for k, (a, b) in enumerate(pairs):
-            offset, group, core, slot = spots[row][k]
-            weight = weights[row][0, k]
-
-            def add(target):
-                at = offset * pieces + slot
-                for mat, source in ((0, full), (1, full2)):
-                    part = (weight * source[cut(a), cut(b)]).astype(bf16).astype(f32)
-                    target[mat, at] = (target[mat, at].astype(f32) + part).astype(target.dtype)
-
-            @pl.when(jnp.logical_and(group == here_group, core == here_core))
-            def _():
-                add(kept)
-
+        for at, mine, mates, part in parts(1, row):
+            add(kept, 1, at, jnp.where(mine, part, 0.0))
             if cores > 1:
-
-                @pl.when(jnp.logical_and(group == here_group, core != here_core))
-                def _():
-                    add(sent)
+                add(sent, 1, at, jnp.where(mates, part, 0.0))
 
 
 def shards(hamilton_blocks, pair_ids, weights, potential):
@@ -219,16 +221,17 @@
     near += [send(hamilton_blocks, same, g) for g in range(1, groups)]
     late = [far_slab]
     late += [send(hamilton_blocks, first, g) for g in range(1, groups)]
-    late += [send(far_slab, same, g) for g in range(1, groups)]
-    near.append(jnp.concatenate(late))
-    ids = [pair_ids] + [send(pair_ids, same, g) for g in range(1, groups)]
-    scales = [weights] + [send(weights, same, g) for g in range(1, groups)]
-    near = [jnp.concatenate(near[:-1]), near[-1]]
+    last = [send(far_slab, same, g) for g in range(1, groups)]
+    own_ids = jnp.pad(pair_ids, ((0, 0), (0, 1)))
+    own_weights = jnp.pad(weights, ((0, 0), (0, 1)))
+    ids = [own_ids] + [send(pair_ids, same, g) for g in range(1, groups)]
+    scales = [own_weights] + [send(weights, same, g) for g in range(1, groups)]
+    near = [jnp.concatenate(part) for part in (near, late, last)]
     blocks = near
     if cores > 1:
-        early = send(near[0], same, 0, 1)
+        early = [send(part, same, 0, 1) for part in near[:2]]
         near, ids, scales = lax.optimization_barrier((near, ids, scales))
-        blocks = near + [early, send(near[1], same, 0, 1)]
+        blocks = near + early + [send(near[2], same, 0, 1)]
 
     sizes = (slabs, groups, cores, pieces, groups, nb, bs)
     smem = pl.BlockSpec(memory_space=pltpu.SMEM)

time: 48.2 us -> 47.9 us (level)
  local copies, waits for them, and re-layouts: 0.96 us -> 2.33 us
  waiting for transfers between devices: 18 us -> 17.3 us
  starting transfers between devices: 18.9 us -> 18.4 us
    pad x0 -> x2, local copies, waits for them, and re-layouts: none -> 1.32 us  [the longest x1 0.66 us: shards(): own_ids = jnp.pad(pair_ids, ((0, 0), (0, 1)))]
    ppermute x12 -> x13, waiting for transfers between devices: 18 us -> 17.3 us  [send(): return lax.ppermute(value, AXES, pairs)]
    ppermute x12 -> x13, starting transfers between devices: 18.9 us -> 18.4 us  [send(): return lax.ppermute(value, AXES, pairs)]
    unnamed x6 -> x3, local copies, waits for them, and re-layouts: 0.94 us -> 0.98 us
  transfers between devices with their start and end apart: 12 -> 13, of which waited for: 7 -> 7; matrix products, arithmetic and copies ran while one was open for 2% -> 5% of each run, Pallas kernels for 0% -> 0%
where the time goes in v2:
time: 47.9 us; the launch traced here: 47.7 us
  starting transfers between devices  18.4 us (38%)
  waiting for transfers between devices  17.3 us (36%)
  Pallas kernels  7.17 us (15%)
  local copies, waits for them, and re-layouts  2.33 us (5%)
  between operations  1.39 us (3%)
  other arithmetic  1.09 us (2%)
    ppermute x13, starting transfers between devices, send(): return lax.ppermute(value, AXES, pairs)  18.4 us
    ppermute x13, waiting for transfers between devices, send(): return lax.ppermute(value, AXES, pairs)  17.3 us
    pallas_call x1, Pallas kernels, shards(): pl.pallas_call(functools.partial(step_kernel, sizes), out_shape=(jax.Shap...  7.17 us
    unnamed x3, local copies, waits for them, and re-layouts  0.98 us
  transfers between devices with their start and end apart: 13, of which 7 were waited for; matrix products, arithmetic and copies ran while one was open for 5% of the time, Pallas kernels for 0%

profile of v2, /device:TPU:0, one launch (start us, length us, event | category | flops | bytes accessed | tf_op | source)
XLA Modules:
  0.0 47.7 jit_solution(265172945428662929)
XLA Ops:
  0.6 3.1 %collective-permute-start = (bf16[4,128,128]{2,1,0:T(8,128)(2,1)}, bf16[4,128,128]{2,1,0:T(8,128)(2,1)S(1)}, u32[]{:S(2)}, u32[]{:S(2)}) collective-permute-start(bf16[4,128,128]{2,1,0:T(8,128)(2,1)} %param.4), channel_id=1, source_target_pairs={{0,4},{1,5},{2,6},{3,7},{4,0},{5,1},{6,2},{7,3},{8,12},{9,13},{10,... | collective-permute-start | bytes 393224 | tf_op jit(solution)/shard_map/ppermute | solution.py:214
  3.7 1.5 %collective-permute-start.1 = (bf16[4,128,128]{2,1,0:T(8,128)(2,1)}, bf16[4,128,128]{2,1,0:T(8,128)(2,1)S(1)}, u32[]{:S(2)}, u32[]{:S(2)}) collective-permute-start(bf16[4,128,128]{2,1,0:T(8,128)(2,1)} %param.4), channel_id=1, source_target_pairs={{0,2},{1,3},{2,0},{3,1},{4,6},{5,7},{6,4},{7,5},{8,10},{9,11},{10,... | collective-permute-start | bytes 393224 | tf_op jit(solution)/shard_map/ppermute | solution.py:214
  5.2 0.0 collective-permute-start.3
  5.2 5.0 %collective-permute-start.2 = (bf16[4,128,128]{2,1,0:T(8,128)(2,1)}, bf16[4,128,128]{2,1,0:T(8,128)(2,1)S(1)}, u32[]{:S(2)}, u32[]{:S(2)}) collective-permute-start(bf16[4,128,128]{2,1,0:T(8,128)(2,1)} %param.4), channel_id=1, source_target_pairs={{0,28},{1,29},{2,30},{3,31},{4,8},{5,9},{6,10},{7,11},{8,4},{9,5},... | collective-permute-start | bytes 393224 | tf_op jit(solution)/shard_map/ppermute | solution.py:214
  10.2 0.9 %constant_dynamic-update-slice_fusion.2 = bf16[12,128,128]{2,1,0:T(8,128)(2,1)S(1)} fusion(bf16[4,128,128]{2,1,0:T(8,128)(2,1)} %param.4), kind=kLoop, calls=%fused_computation.11 | loop fusion | bytes 262144
  11.2 0.0 collective-permute-done
  11.2 0.0 collective-permute-done.1
  11.2 0.1 collective-permute-start.7
  11.3 2.9 %collective-permute-done.2 = bf16[4,128,128]{2,1,0:T(8,128)(2,1)S(1)} collective-permute-done((bf16[4,128,128]{2,1,0:T(8,128)(2,1)}, bf16[4,128,128]{2,1,0:T(8,128)(2,1)S(1)}, u32[]{:S(2)}, u32[]{:S(2)}) %collective-permute-start.2) | collective-permute-done | bytes 131104 | tf_op jit(solution)/shard_map/ppermute | solution.py:214
  14.3 1.6 %collective-permute-start.4 = (bf16[4,128,128]{2,1,0:T(8,128)(2,1)S(1)}, bf16[4,128,128]{2,1,0:T(8,128)(2,1)S(1)}, u32[]{:S(2)}, u32[]{:S(2)}) collective-permute-start(bf16[4,128,128]{2,1,0:T(8,128)(2,1)S(1)} %collective-permute-done.2), channel_id=1, source_target_pairs={{0,2},{1,3},{2,0},{3,1},{4,6},{5,7},{6,4},{7,5},{8,10},{9,11},{10,... | collective-permute-start | bytes 393224 | tf_op jit(solution)/shard_map/ppermute | solution.py:214
  15.9 0.0 collective-permute-done.3
  16.0 0.1 collective-permute-start.8
  16.0 0.5 collective-permute-start.5
  16.5 1.6 %collective-permute-start.6 = (f32[1,10]{1,0:T(1,128)}, f32[1,10]{1,0:T(1,128)S(1)}, u32[]{:S(2)}, u32[]{:S(2)}) collective-permute-start(f32[1,10]{1,0:T(1,128)} %param.6), channel_id=1, source_target_pairs={{0,2},{1,3},{2,0},{3,1},{4,6},{5,7},{6,4},{7,5},{8,10},{9,11},{10,... | collective-permute-start | bytes 128 | tf_op jit(solution)/shard_map/ppermute | solution.py:214
  18.1 0.7 %pad.8.refs_0_ = s32[1,11]{1,0:T(1,128)S(1)} pad(s32[1,10]{1,0:T(1,128)} %param.5, s32[]{:T(128)} %constant.2.clone.1), padding=0_0x0_1 | pad | bytes 88 | tf_op jit(solution)/shard_map/jit(_pad)/pad | solution.py:225
  18.8 0.7 %pad.9.refs_2_ = f32[1,11]{1,0:T(1,128)S(1)} pad(f32[1,10]{1,0:T(1,128)} %param.6, f32[]{:T(128)} %constant.3.clone.1), padding=0_0x0_1 | pad | bytes 88 | tf_op jit(solution)/shard_map/jit(_pad)/pad | solution.py:226
  19.5 0.4 collective-permute-done.5.refs_1_
  19.8 0.4 collective-permute-done.6.refs_3_
  20.2 0.0 collective-permute-done.4.refs_7_
  20.2 0.0 collective-permute-start.9
  20.9 0.0 collective-permute-done.8.refs_9_
  20.9 0.7 %collective-permute-done.9.refs_10_ = bf16[4,128,128]{2,1,0:T(8,128)(2,1)S(1)} collective-permute-done((bf16[4,128,128]{2,1,0:T(8,128)(2,1)S(1)}, bf16[4,128,128]{2,1,0:T(8,128)(2,1)S(1)}, u32[]{:S(2)}, u32[]{:S(2)}) %collective-permute-start.9) | collective-permute-done | bytes 131104 | tf_op jit(solution)/shard_map/ppermute | solution.py:214
  21.5 0.0 collective-permute-done.7.refs_8_
  21.6 7.2 %submatrix_step.1 = (f32[2,12,128,128]{3,2,1,0:T(8,128)S(1)}, bf16[2,12,128,128]{3,2,1,0:T(8,128)(2,1)S(1)}) custom-call(s32[1,11]{1,0:T(1,128)S(1)} %pad.8.refs_0_, s32[1,10]{1,0:T(1,128)S(1)} %collective-permute-done.5.refs_1_, f32[1,11]{1,0:T(1,128)S(1)} %pad.9.refs_2_, f32[1,10]{1,0:T(1,128)S(1)} %collective-permute-done.6.refs_3_, f32[1]{0:T(128)S(6)} %copy.9.refs_4_, ...), custom_call_target="tpu_custom_call" | custom-call | tf_op jit(solution)/shard_map/submatrix_step/pallas_call | solution.py:242
  28.7 0.2 collective-permute-start.10
  28.9 2.1 %collective-permute-done.10 = bf16[2,12,128,128]{3,2,1,0:T(8,128)(2,1)S(1)} collective-permute-done((bf16[2,12,128,128]{3,2,1,0:T(8,128)(2,1)S(1)}, bf16[2,12,128,128]{3,2,1,0:T(8,128)(2,1)S(1)}, u32[]{:S(2)}, u32[]{:S(2)}) %collective-permute-start.10) | collective-permute-done | bytes 786464 | tf_op jit(solution)/shard_map/ppermute | solution.py:214
  31.1 0.2 add_convert_fusion.1
  31.3 4.7 %collective-permute-start.11 = (bf16[2,4,128,128]{3,2,1,0:T(8,128)(2,1)S(1)}, bf16[2,4,128,128]{3,2,1,0:T(8,128)(2,1)S(1)}, u32[]{:S(2)}, u32[]{:S(2)}) collective-permute-start(bf16[2,4,128,128]{3,2,1,0:T(8,128)(2,1)S(1)} %get-tuple-element.20), channel_id=1, source_target_pairs={{0,28},{1,29},{2,30},{3,31},{4,0},{5,1},{6,2},{7,3},{8,4},{9,5},{1... | collective-permute-start | bytes 786440 | tf_op jit(solution)/shard_map/ppermute | solution.py:214
  36.0 0.0 collective-permute-start.12
  36.0 5.9 %collective-permute-done.11 = bf16[2,4,128,128]{3,2,1,0:T(8,128)(2,1)S(1)} collective-permute-done((bf16[2,4,128,128]{3,2,1,0:T(8,128)(2,1)S(1)}, bf16[2,4,128,128]{3,2,1,0:T(8,128)(2,1)S(1)}, u32[]{:S(2)}, u32[]{:S(2)}) %collective-permute-start.11) | collective-permute-done | bytes 262176 | tf_op jit(solution)/shard_map/ppermute | solution.py:214
  41.9 4.9 %collective-permute-done.12 = bf16[2,4,128,128]{3,2,1,0:T(8,128)(2,1)S(1)} collective-permute-done((bf16[2,4,128,128]{3,2,1,0:T(8,128)(2,1)S(1)}, bf16[2,4,128,128]{3,2,1,0:T(8,128)(2,1)S(1)}, u32[]{:S(2)}, u32[]{:S(2)}) %collective-permute-start.12) | collective-permute-done | bytes 262176 | tf_op jit(solution)/shard_map/ppermute | solution.py:214
  46.8 0.9 %fusion.1 = (f32[4,128,128]{2,1,0:T(8,128)}, f32[4,128,128]{2,1,0:T(8,128)}) fusion(f32[2,4,128,128]{3,2,1,0:T(8,128)S(1)} %get-tuple-element.22, bf16[2,4,128,128]{3,2,1,0:T(8,128)(2,1)S(1)} %collective-permute-done.12, bf16[2,4,128,128]{3,2,1,0:T(8,128)(2,1)S(1)} %collective-permute-done.11), kind=kLoop, calls=%fused_computation.5 | loop fusion | flops 524288 | bytes 1572864 | tf_op jit(solution)/shard_map/add | solution.py:270
  (4 shorter events, 0.1 us)
Async XLA Ops:
  0.6 10.5 %collective-permute-start = (bf16[4,128,128]{2,1,0:T(8,128)(2,1)}, bf16[4,128,128]{2,1,0:T(8,128)(2,1)S(1)}, u32[]{:S(2)}, u32[]{:S(2)}) collective-permute-start(bf16[4,128,128]{2,1,0:T(8,128)(2,1)} %param.4), channel_id=1, source_target_pairs={{0,4},{1,5},{2,6},{3,7},{4,0},{5,1},{6,2},{7,3},{8,12},{9,13},{10,... | collective-permute-start | bytes 393224 | tf_op jit(solution)/shard_map/ppermute | solution.py:214
  3.7 7.5 %collective-permute-start.1 = (bf16[4,128,128]{2,1,0:T(8,128)(2,1)}, bf16[4,128,128]{2,1,0:T(8,128)(2,1)S(1)}, u32[]{:S(2)}, u32[]{:S(2)}) collective-permute-start(bf16[4,128,128]{2,1,0:T(8,128)(2,1)} %param.4), channel_id=1, source_target_pairs={{0,2},{1,3},{2,0},{3,1},{4,6},{5,7},{6,4},{7,5},{8,10},{9,11},{10,... | collective-permute-start | bytes 393224 | tf_op jit(solution)/shard_map/ppermute | solution.py:214
  5.2 10.7 %collective-permute-start.3 = (bf16[4,128,128]{2,1,0:T(8,128)(2,1)}, bf16[4,128,128]{2,1,0:T(8,128)(2,1)S(1)}, u32[]{:S(2)}, u32[]{:S(2)}) collective-permute-start(bf16[4,128,128]{2,1,0:T(8,128)(2,1)} %param.4), channel_id=1, source_target_pairs={{0,6},{1,7},{2,4},{3,5},{4,2},{5,3},{6,0},{7,1},{8,14},{9,15},{10,... | collective-permute-start | bytes 393224 | tf_op jit(solution)/shard_map/ppermute | solution.py:214
  5.2 9.0 %collective-permute-start.2 = (bf16[4,128,128]{2,1,0:T(8,128)(2,1)}, bf16[4,128,128]{2,1,0:T(8,128)(2,1)S(1)}, u32[]{:S(2)}, u32[]{:S(2)}) collective-permute-start(bf16[4,128,128]{2,1,0:T(8,128)(2,1)} %param.4), channel_id=1, source_target_pairs={{0,28},{1,29},{2,30},{3,31},{4,8},{5,9},{6,10},{7,11},{8,4},{9,5},... | collective-permute-start | bytes 393224 | tf_op jit(solution)/shard_map/ppermute | solution.py:214
  11.2 10.3 %collective-permute-start.7 = (bf16[12,128,128]{2,1,0:T(8,128)(2,1)S(1)}, bf16[12,128,128]{2,1,0:T(8,128)(2,1)S(1)}, u32[]{:S(2)}, u32[]{:S(2)}) collective-permute-start(bf16[12,128,128]{2,1,0:T(8,128)(2,1)S(1)} %constant_dynamic-update-slice_fusion.refs_5_), channel_id=1, source_target_pairs={{0,1},{1,0},{2,3},{3,2},{4,5},{5,4},{6,7},{7,6},{8,9},{9,8},{10,11... | collective-permute-start | bytes 1179656 | tf_op jit(solution)/shard_map/ppermute | solution.py:214
  14.3 5.9 %collective-permute-start.4 = (bf16[4,128,128]{2,1,0:T(8,128)(2,1)S(1)}, bf16[4,128,128]{2,1,0:T(8,128)(2,1)S(1)}, u32[]{:S(2)}, u32[]{:S(2)}) collective-permute-start(bf16[4,128,128]{2,1,0:T(8,128)(2,1)S(1)} %collective-permute-done.2), channel_id=1, source_target_pairs={{0,2},{1,3},{2,0},{3,1},{4,6},{5,7},{6,4},{7,5},{8,10},{9,11},{10,... | collective-permute-start | bytes 393224 | tf_op jit(solution)/shard_map/ppermute | solution.py:214
  16.0 4.9 %collective-permute-start.8 = (bf16[8,128,128]{2,1,0:T(8,128)(2,1)S(1)}, bf16[8,128,128]{2,1,0:T(8,128)(2,1)S(1)}, u32[]{:S(2)}, u32[]{:S(2)}) collective-permute-start(bf16[8,128,128]{2,1,0:T(8,128)(2,1)S(1)} %constant_dynamic-update-slice_fusion.3.refs_6_), channel_id=1, source_target_pairs={{0,1},{1,0},{2,3},{3,2},{4,5},{5,4},{6,7},{7,6},{8,9},{9,8},{10,11... | collective-permute-start | bytes 786440 | tf_op jit(solution)/shard_map/ppermute | solution.py:214
  16.0 3.8 %collective-permute-start.5 = (s32[1,10]{1,0:T(1,128)}, s32[1,10]{1,0:T(1,128)S(1)}, u32[]{:S(2)}, u32[]{:S(2)}) collective-permute-start(s32[1,10]{1,0:T(1,128)} %param.5), channel_id=1, source_target_pairs={{0,2},{1,3},{2,0},{3,1},{4,6},{5,7},{6,4},{7,5},{8,10},{9,11},{10,... | collective-permute-start | bytes 128 | tf_op jit(solution)/shard_map/ppermute | solution.py:214
  16.5 3.7 %collective-permute-start.6 = (f32[1,10]{1,0:T(1,128)}, f32[1,10]{1,0:T(1,128)S(1)}, u32[]{:S(2)}, u32[]{:S(2)}) collective-permute-start(f32[1,10]{1,0:T(1,128)} %param.6), channel_id=1, source_target_pairs={{0,2},{1,3},{2,0},{3,1},{4,6},{5,7},{6,4},{7,5},{8,10},{9,11},{10,... | collective-permute-start | bytes 128 | tf_op jit(solution)/shard_map/ppermute | solution.py:214
  20.2 1.3 %collective-permute-start.9 = (bf16[4,128,128]{2,1,0:T(8,128)(2,1)S(1)}, bf16[4,128,128]{2,1,0:T(8,128)(2,1)S(1)}, u32[]{:S(2)}, u32[]{:S(2)}) collective-permute-start(bf16[4,128,128]{2,1,0:T(8,128)(2,1)S(1)} %collective-permute-done.4.refs_7_), channel_id=1, source_target_pairs={{0,1},{1,0},{2,3},{3,2},{4,5},{5,4},{6,7},{7,6},{8,9},{9,8},{10,11... | collective-permute-start | bytes 393224 | tf_op jit(solution)/shard_map/ppermute | solution.py:214
  28.7 2.4 %collective-permute-start.10 = (bf16[2,12,128,128]{3,2,1,0:T(8,128)(2,1)S(1)}, bf16[2,12,128,128]{3,2,1,0:T(8,128)(2,1)S(1)}, u32[]{:S(2)}, u32[]{:S(2)}) collective-permute-start(bf16[2,12,128,128]{3,2,1,0:T(8,128)(2,1)S(1)} %get-tuple-element.19), channel_id=1, source_target_pairs={{0,1},{1,0},{2,3},{3,2},{4,5},{5,4},{6,7},{7,6},{8,9},{9,8},{10,11... | collective-permute-start | bytes 2359304 | tf_op jit(solution)/shard_map/ppermute | solution.py:214
  31.3 10.6 %collective-permute-start.11 = (bf16[2,4,128,128]{3,2,1,0:T(8,128)(2,1)S(1)}, bf16[2,4,128,128]{3,2,1,0:T(8,128)(2,1)S(1)}, u32[]{:S(2)}, u32[]{:S(2)}) collective-permute-start(bf16[2,4,128,128]{3,2,1,0:T(8,128)(2,1)S(1)} %get-tuple-element.20), channel_id=1, source_target_pairs={{0,28},{1,29},{2,30},{3,31},{4,0},{5,1},{6,2},{7,3},{8,4},{9,5},{1... | collective-permute-start | bytes 786440 | tf_op jit(solution)/shard_map/ppermute | solution.py:214
  36.0 10.8 %collective-permute-start.12 = (bf16[2,4,128,128]{3,2,1,0:T(8,128)(2,1)S(1)}, bf16[2,4,128,128]{3,2,1,0:T(8,128)(2,1)S(1)}, u32[]{:S(2)}, u32[]{:S(2)}) collective-permute-start(bf16[2,4,128,128]{3,2,1,0:T(8,128)(2,1)S(1)} %get-tuple-element.21), channel_id=1, source_target_pairs={{0,4},{1,5},{2,6},{3,7},{4,8},{5,9},{6,10},{7,11},{8,12},{9,13},{1... | collective-permute-start | bytes 786440 | tf_op jit(solution)/shard_map/ppermute | solution.py:214

commit v3 on v2

--- a/solution.py
+++ b/solution.py
@@ -168,16 +168,17 @@
             same_group = group == here_group
             mine = jnp.logical_and(same_group, core == here_core)
             mates = jnp.logical_and(same_group, core != here_core)
-            yield offset * pieces + slot, mine, mates, part.astype(bf16).astype(f32)
-
-    def add(target, mat, at, part):
-        target[mat, at] = (target[mat, at].astype(f32) + part).astype(target.dtype)
-
-    for row in range(rows):
-        for at, mine, mates, part in parts(0, row):
-            add(kept, 0, at, jnp.where(mine, part, 0.0))
+            turned = jnp.where(offset == 1, 2, offset // 2) * pieces + slot
+            yield offset * pieces + slot, turned, mine, mates, part.astype(bf16).astype(f32)
+
+    def add(target, where, part):
+        target[where] = (target[where].astype(f32) + part).astype(target.dtype)
+
+    for row in range(rows):
+        for at, turned, mine, mates, part in parts(0, row):
+            add(kept, (0, at), jnp.where(mine, part, 0.0))
             if cores > 1:
-                add(sent, 0, at, jnp.where(mates, part, 0.0))
+                add(sent, (turned, 0), jnp.where(mates, part, 0.0))
     for i, row, upper, right in strips():
         base_hi, base_lo, _, _, a_hi, a_lo, _, _, _, full2 = state[row]
         value = mm(a_hi[upper, :], base_hi[:, right]) + mm(a_lo[upper, :], base_hi[:, right])
@@ -187,10 +188,10 @@
         )
         full2[upper, right] = value
     for row in range(rows):
-        for at, mine, mates, part in parts(1, row):
-            add(kept, 1, at, jnp.where(mine, part, 0.0))
+        for at, turned, mine, mates, part in parts(1, row):
+            add(kept, (1, at), jnp.where(mine, part, 0.0))
             if cores > 1:
-                add(sent, 1, at, jnp.where(mates, part, 0.0))
+                add(sent, (turned, 1), jnp.where(mates, part, 0.0))
 
 
 def shards(hamilton_blocks, pair_ids, weights, potential):
@@ -243,7 +244,7 @@
         functools.partial(step_kernel, sizes),
         out_shape=(
             jax.ShapeDtypeStruct((2, slots, bs, bs), f32),
-            jax.ShapeDtypeStruct((2, slots, bs, bs), bf16),
+            jax.ShapeDtypeStruct((slots, 2, bs, bs), bf16),
         ),
         in_specs=[smem] * (2 * groups + 1) + [vmem] * len(blocks),
         out_specs=(vmem, vmem),
@@ -261,13 +262,17 @@
     )(*ids, *scales, potential, *blocks)
     kept = [kept[:, i * pieces : (i + 1) * pieces] for i in range(3)]
     if cores > 1:
-        other = send(sent, same, 0, 1)
-        kept = [
-            part + other[:, i * pieces : (i + 1) * pieces].astype(f32) for i, part in enumerate(kept)
-        ]
+        leaving = jnp.swapaxes(send(sent[: 2 * pieces], same, 0, 1), 0, 1)
+        staying = send(sent[2 * pieces :], same, 0, 1)
+        kept[0] += leaving[:, :pieces].astype(f32)
+        kept[2] += leaving[:, pieces:].astype(f32)
     below = send(kept[0].astype(bf16), lambda s: s - 1)
     above = send(kept[2].astype(bf16), lambda s: s + 1)
-    return tuple(kept[1][i] + below[i].astype(f32) + above[i].astype(f32) for i in range(2))
+    last = [below, above]
+    if cores > 1:
+        last = lax.optimization_barrier(last + [staying])
+        last[2] = jnp.swapaxes(last[2], 0, 1)
+    return tuple(kept[1][i] + sum(part[i].astype(f32) for part in last) for i in range(2))
 
 
 def solution(mesh):

time: 47.9 us -> 46.5 us (0.971)
  waiting for transfers between devices: 17.3 us -> 15.4 us
  starting transfers between devices: 18.4 us -> 18.9 us
    ppermute x13 -> x14, waiting for transfers between devices: 17.3 us -> 15.4 us  [send(): return lax.ppermute(value, AXES, pairs)]
    ppermute x13 -> x14, starting transfers between devices: 18.4 us -> 18.9 us  [send(): return lax.ppermute(value, AXES, pairs)]
  transfers between devices with their start and end apart: 13 -> 14, of which waited for: 7 -> 7; matrix products, arithmetic and copies ran while one was open for 5% -> 5% of each run, Pallas kernels for 0% -> 0%
where the time goes in v3:
time: 46.5 us; the launch traced here: 46.4 us
  starting transfers between devices  18.9 us (41%)
  waiting for transfers between devices  15.4 us (33%)
  Pallas kernels  7.26 us (16%)
  local copies, waits for them, and re-layouts  2.39 us (5%)
  between operations  1.4 us (3%)
  other arithmetic  1.03 us (2%)
    ppermute x14, starting transfers between devices, send(): return lax.ppermute(value, AXES, pairs)  18.9 us
    ppermute x14, waiting for transfers between devices, send(): return lax.ppermute(value, AXES, pairs)  15.4 us
    pallas_call x1, Pallas kernels, shards(): pl.pallas_call(functools.partial(step_kernel, sizes), out_shape=(jax.Shap...  7.26 us
    unnamed x3, local copies, waits for them, and re-layouts  0.98 us
  transfers between devices with their start and end apart: 14, of which 7 were waited for; matrix products, arithmetic and copies ran while one was open for 5% of the time, Pallas kernels for 0%

profile of v3, /device:TPU:0, one launch (start us, length us, event | category | flops | bytes accessed | tf_op | source)
XLA Modules:
  0.0 46.4 jit_solution(11804154213067351337)
XLA Ops:
  0.6 3.1 %collective-permute-start = (bf16[4,128,128]{2,1,0:T(8,128)(2,1)}, bf16[4,128,128]{2,1,0:T(8,128)(2,1)S(1)}, u32[]{:S(2)}, u32[]{:S(2)}) collective-permute-start(bf16[4,128,128]{2,1,0:T(8,128)(2,1)} %param.4), channel_id=1, source_target_pairs={{0,4},{1,5},{2,6},{3,7},{4,0},{5,1},{6,2},{7,3},{8,12},{9,13},{10,... | collective-permute-start | bytes 393224 | tf_op jit(solution)/shard_map/ppermute | solution.py:215
  3.7 1.5 %collective-permute-start.1 = (bf16[4,128,128]{2,1,0:T(8,128)(2,1)}, bf16[4,128,128]{2,1,0:T(8,128)(2,1)S(1)}, u32[]{:S(2)}, u32[]{:S(2)}) collective-permute-start(bf16[4,128,128]{2,1,0:T(8,128)(2,1)} %param.4), channel_id=1, source_target_pairs={{0,2},{1,3},{2,0},{3,1},{4,6},{5,7},{6,4},{7,5},{8,10},{9,11},{10,... | collective-permute-start | bytes 393224 | tf_op jit(solution)/shard_map/ppermute | solution.py:215
  5.2 0.0 collective-permute-start.3
  5.2 5.0 %collective-permute-start.2 = (bf16[4,128,128]{2,1,0:T(8,128)(2,1)}, bf16[4,128,128]{2,1,0:T(8,128)(2,1)S(1)}, u32[]{:S(2)}, u32[]{:S(2)}) collective-permute-start(bf16[4,128,128]{2,1,0:T(8,128)(2,1)} %param.4), channel_id=1, source_target_pairs={{0,28},{1,29},{2,30},{3,31},{4,8},{5,9},{6,10},{7,11},{8,4},{9,5},... | collective-permute-start | bytes 393224 | tf_op jit(solution)/shard_map/ppermute | solution.py:215
  10.2 0.9 %constant_dynamic-update-slice_fusion.2 = bf16[12,128,128]{2,1,0:T(8,128)(2,1)S(1)} fusion(bf16[4,128,128]{2,1,0:T(8,128)(2,1)} %param.4), kind=kLoop, calls=%fused_computation.10 | loop fusion | bytes 262144
  11.2 0.0 collective-permute-done
  11.2 0.0 collective-permute-done.1
  11.2 0.1 collective-permute-start.7
  11.3 2.9 %collective-permute-done.2 = bf16[4,128,128]{2,1,0:T(8,128)(2,1)S(1)} collective-permute-done((bf16[4,128,128]{2,1,0:T(8,128)(2,1)}, bf16[4,128,128]{2,1,0:T(8,128)(2,1)S(1)}, u32[]{:S(2)}, u32[]{:S(2)}) %collective-permute-start.2) | collective-permute-done | bytes 131104 | tf_op jit(solution)/shard_map/ppermute | solution.py:215
  14.3 1.6 %collective-permute-start.4 = (bf16[4,128,128]{2,1,0:T(8,128)(2,1)S(1)}, bf16[4,128,128]{2,1,0:T(8,128)(2,1)S(1)}, u32[]{:S(2)}, u32[]{:S(2)}) collective-permute-start(bf16[4,128,128]{2,1,0:T(8,128)(2,1)S(1)} %collective-permute-done.2), channel_id=1, source_target_pairs={{0,2},{1,3},{2,0},{3,1},{4,6},{5,7},{6,4},{7,5},{8,10},{9,11},{10,... | collective-permute-start | bytes 393224 | tf_op jit(solution)/shard_map/ppermute | solution.py:215
  15.9 0.0 collective-permute-done.3
  16.0 0.1 collective-permute-start.8
  16.0 0.5 collective-permute-start.5
  16.5 1.6 %collective-permute-start.6 = (f32[1,10]{1,0:T(1,128)}, f32[1,10]{1,0:T(1,128)S(1)}, u32[]{:S(2)}, u32[]{:S(2)}) collective-permute-start(f32[1,10]{1,0:T(1,128)} %param.6), channel_id=1, source_target_pairs={{0,2},{1,3},{2,0},{3,1},{4,6},{5,7},{6,4},{7,5},{8,10},{9,11},{10,... | collective-permute-start | bytes 128 | tf_op jit(solution)/shard_map/ppermute | solution.py:215
  18.1 0.7 %pad.8.refs_0_ = s32[1,11]{1,0:T(1,128)S(1)} pad(s32[1,10]{1,0:T(1,128)} %param.5, s32[]{:T(128)} %constant.2.clone.1), padding=0_0x0_1 | pad | bytes 88 | tf_op jit(solution)/shard_map/jit(_pad)/pad | solution.py:226
  18.8 0.7 %pad.9.refs_2_ = f32[1,11]{1,0:T(1,128)S(1)} pad(f32[1,10]{1,0:T(1,128)} %param.6, f32[]{:T(128)} %constant.3.clone.1), padding=0_0x0_1 | pad | bytes 88 | tf_op jit(solution)/shard_map/jit(_pad)/pad | solution.py:227
  19.5 0.4 collective-permute-done.5.refs_1_
  19.8 0.4 collective-permute-done.6.refs_3_
  20.2 0.0 collective-permute-done.4.refs_7_
  20.2 0.0 collective-permute-start.9
  20.9 0.0 collective-permute-done.8.refs_9_
  20.9 0.7 %collective-permute-done.9.refs_10_ = bf16[4,128,128]{2,1,0:T(8,128)(2,1)S(1)} collective-permute-done((bf16[4,128,128]{2,1,0:T(8,128)(2,1)S(1)}, bf16[4,128,128]{2,1,0:T(8,128)(2,1)S(1)}, u32[]{:S(2)}, u32[]{:S(2)}) %collective-permute-start.9) | collective-permute-done | bytes 131104 | tf_op jit(solution)/shard_map/ppermute | solution.py:215
  21.5 0.0 collective-permute-done.7.refs_8_
  21.6 7.3 %submatrix_step.1 = (f32[2,12,128,128]{3,2,1,0:T(8,128)S(1)}, bf16[12,2,128,128]{3,2,1,0:T(8,128)(2,1)S(1)}) custom-call(s32[1,11]{1,0:T(1,128)S(1)} %pad.8.refs_0_, s32[1,10]{1,0:T(1,128)S(1)} %collective-permute-done.5.refs_1_, f32[1,11]{1,0:T(1,128)S(1)} %pad.9.refs_2_, f32[1,10]{1,0:T(1,128)S(1)} %collective-permute-done.6.refs_3_, f32[1]{0:T(128)S(6)} %copy.17.refs_4_, ...), custom_call_target="tpu_custom_call" | custom-call | tf_op jit(solution)/shard_map/submatrix_step/pallas_call | solution.py:243
  28.9 0.2 collective-permute-start.10
  29.1 0.4 collective-permute-start.13
  29.5 1.3 %collective-permute-done.10 = bf16[8,2,128,128]{3,2,1,0:T(8,128)(2,1)S(1)} collective-permute-done((bf16[8,2,128,128]{3,2,1,0:T(8,128)(2,1)S(1)}, bf16[8,2,128,128]{3,2,1,0:T(8,128)(2,1)S(1)}, u32[]{:S(2)}, u32[]{:S(2)}) %collective-permute-start.10) | collective-permute-done | bytes 524320 | tf_op jit(solution)/shard_map/ppermute | solution.py:215
  30.8 0.1 fusion
  31.0 0.8 %collective-permute-start.12 = (bf16[2,4,128,128]{3,2,0,1:T(8,128)(2,1)S(1)}, bf16[2,4,128,128]{3,2,0,1:T(8,128)(2,1)S(1)}, u32[]{:S(2)}, u32[]{:S(2)}) collective-permute-start(bf16[2,4,128,128]{3,2,0,1:T(8,128)(2,1)S(1)} %get-tuple-element.28), channel_id=1, source_target_pairs={{0,4},{1,5},{2,6},{3,7},{4,8},{5,9},{6,10},{7,11},{8,12},{9,13},{1... | collective-permute-start | bytes 786440 | tf_op jit(solution)/shard_map/ppermute | solution.py:215
  31.8 4.0 %collective-permute-start.11 = (bf16[2,4,128,128]{3,2,0,1:T(8,128)(2,1)S(1)}, bf16[2,4,128,128]{3,2,0,1:T(8,128)(2,1)S(1)}, u32[]{:S(2)}, u32[]{:S(2)}) collective-permute-start(bf16[2,4,128,128]{3,2,0,1:T(8,128)(2,1)S(1)} %get-tuple-element.29), channel_id=1, source_target_pairs={{0,28},{1,29},{2,30},{3,31},{4,0},{5,1},{6,2},{7,3},{8,4},{9,5},{1... | collective-permute-start | bytes 786440 | tf_op jit(solution)/shard_map/ppermute | solution.py:215
  35.8 0.0 collective-permute-done.13
  35.8 7.5 %collective-permute-done.12 = bf16[2,4,128,128]{3,2,0,1:T(8,128)(2,1)S(1)} collective-permute-done((bf16[2,4,128,128]{3,2,0,1:T(8,128)(2,1)S(1)}, bf16[2,4,128,128]{3,2,0,1:T(8,128)(2,1)S(1)}, u32[]{:S(2)}, u32[]{:S(2)}) %collective-permute-start.12) | collective-permute-done | bytes 262176 | tf_op jit(solution)/shard_map/ppermute | solution.py:215
  43.3 2.2 %collective-permute-done.11 = bf16[2,4,128,128]{3,2,0,1:T(8,128)(2,1)S(1)} collective-permute-done((bf16[2,4,128,128]{3,2,0,1:T(8,128)(2,1)S(1)}, bf16[2,4,128,128]{3,2,0,1:T(8,128)(2,1)S(1)}, u32[]{:S(2)}, u32[]{:S(2)}) %collective-permute-start.11) | collective-permute-done | bytes 262176 | tf_op jit(solution)/shard_map/ppermute | solution.py:215
  45.5 0.9 %fusion.2 = (f32[4,128,128]{2,1,0:T(8,128)}, f32[4,128,128]{2,1,0:T(8,128)}) fusion(bf16[2,4,128,128]{3,2,0,1:T(8,128)(2,1)S(1)} %bitcast.7, bf16[2,4,128,128]{3,2,0,1:T(8,128)(2,1)S(1)} %collective-permute-done.12, bf16[2,4,128,128]{3,2,0,1:T(8,128)(2,1)S(1)} %collective-permute-done.11, f32[2,12,128,128]{3,2,1,0:T(8,128)S(1)} %get-tuple-element.21), kind=kLoop, calls=%fused_computation.5 | loop fusion | flops 786432 | bytes 1835008 | tf_op jit(solution)/shard_map/add | solution.py:275
  (6 shorter events, 0.1 us)
Async XLA Ops:
  0.6 10.5 %collective-permute-start = (bf16[4,128,128]{2,1,0:T(8,128)(2,1)}, bf16[4,128,128]{2,1,0:T(8,128)(2,1)S(1)}, u32[]{:S(2)}, u32[]{:S(2)}) collective-permute-start(bf16[4,128,128]{2,1,0:T(8,128)(2,1)} %param.4), channel_id=1, source_target_pairs={{0,4},{1,5},{2,6},{3,7},{4,0},{5,1},{6,2},{7,3},{8,12},{9,13},{10,... | collective-permute-start | bytes 393224 | tf_op jit(solution)/shard_map/ppermute | solution.py:215
  3.7 7.5 %collective-permute-start.1 = (bf16[4,128,128]{2,1,0:T(8,128)(2,1)}, bf16[4,128,128]{2,1,0:T(8,128)(2,1)S(1)}, u32[]{:S(2)}, u32[]{:S(2)}) collective-permute-start(bf16[4,128,128]{2,1,0:T(8,128)(2,1)} %param.4), channel_id=1, source_target_pairs={{0,2},{1,3},{2,0},{3,1},{4,6},{5,7},{6,4},{7,5},{8,10},{9,11},{10,... | collective-permute-start | bytes 393224 | tf_op jit(solution)/shard_map/ppermute | solution.py:215
  5.2 10.7 %collective-permute-start.3 = (bf16[4,128,128]{2,1,0:T(8,128)(2,1)}, bf16[4,128,128]{2,1,0:T(8,128)(2,1)S(1)}, u32[]{:S(2)}, u32[]{:S(2)}) collective-permute-start(bf16[4,128,128]{2,1,0:T(8,128)(2,1)} %param.4), channel_id=1, source_target_pairs={{0,6},{1,7},{2,4},{3,5},{4,2},{5,3},{6,0},{7,1},{8,14},{9,15},{10,... | collective-permute-start | bytes 393224 | tf_op jit(solution)/shard_map/ppermute | solution.py:215
  5.2 9.0 %collective-permute-start.2 = (bf16[4,128,128]{2,1,0:T(8,128)(2,1)}, bf16[4,128,128]{2,1,0:T(8,128)(2,1)S(1)}, u32[]{:S(2)}, u32[]{:S(2)}) collective-permute-start(bf16[4,128,128]{2,1,0:T(8,128)(2,1)} %param.4), channel_id=1, source_target_pairs={{0,28},{1,29},{2,30},{3,31},{4,8},{5,9},{6,10},{7,11},{8,4},{9,5},... | collective-permute-start | bytes 393224 | tf_op jit(solution)/shard_map/ppermute | solution.py:215
  11.2 10.3 %collective-permute-start.7 = (bf16[12,128,128]{2,1,0:T(8,128)(2,1)S(1)}, bf16[12,128,128]{2,1,0:T(8,128)(2,1)S(1)}, u32[]{:S(2)}, u32[]{:S(2)}) collective-permute-start(bf16[12,128,128]{2,1,0:T(8,128)(2,1)S(1)} %constant_dynamic-update-slice_fusion.refs_5_), channel_id=1, source_target_pairs={{0,1},{1,0},{2,3},{3,2},{4,5},{5,4},{6,7},{7,6},{8,9},{9,8},{10,11... | collective-permute-start | bytes 1179656 | tf_op jit(solution)/shard_map/ppermute | solution.py:215
  14.3 5.9 %collective-permute-start.4 = (bf16[4,128,128]{2,1,0:T(8,128)(2,1)S(1)}, bf16[4,128,128]{2,1,0:T(8,128)(2,1)S(1)}, u32[]{:S(2)}, u32[]{:S(2)}) collective-permute-start(bf16[4,128,128]{2,1,0:T(8,128)(2,1)S(1)} %collective-permute-done.2), channel_id=1, source_target_pairs={{0,2},{1,3},{2,0},{3,1},{4,6},{5,7},{6,4},{7,5},{8,10},{9,11},{10,... | collective-permute-start | bytes 393224 | tf_op jit(solution)/shard_map/ppermute | solution.py:215
  16.0 4.9 %collective-permute-start.8 = (bf16[8,128,128]{2,1,0:T(8,128)(2,1)S(1)}, bf16[8,128,128]{2,1,0:T(8,128)(2,1)S(1)}, u32[]{:S(2)}, u32[]{:S(2)}) collective-permute-start(bf16[8,128,128]{2,1,0:T(8,128)(2,1)S(1)} %constant_dynamic-update-slice_fusion.3.refs_6_), channel_id=1, source_target_pairs={{0,1},{1,0},{2,3},{3,2},{4,5},{5,4},{6,7},{7,6},{8,9},{9,8},{10,11... | collective-permute-start | bytes 786440 | tf_op jit(solution)/shard_map/ppermute | solution.py:215
  16.0 3.8 %collective-permute-start.5 = (s32[1,10]{1,0:T(1,128)}, s32[1,10]{1,0:T(1,128)S(1)}, u32[]{:S(2)}, u32[]{:S(2)}) collective-permute-start(s32[1,10]{1,0:T(1,128)} %param.5), channel_id=1, source_target_pairs={{0,2},{1,3},{2,0},{3,1},{4,6},{5,7},{6,4},{7,5},{8,10},{9,11},{10,... | collective-permute-start | bytes 128 | tf_op jit(solution)/shard_map/ppermute | solution.py:215
  16.5 3.7 %collective-permute-start.6 = (f32[1,10]{1,0:T(1,128)}, f32[1,10]{1,0:T(1,128)S(1)}, u32[]{:S(2)}, u32[]{:S(2)}) collective-permute-start(f32[1,10]{1,0:T(1,128)} %param.6), channel_id=1, source_target_pairs={{0,2},{1,3},{2,0},{3,1},{4,6},{5,7},{6,4},{7,5},{8,10},{9,11},{10,... | collective-permute-start | bytes 128 | tf_op jit(solution)/shard_map/ppermute | solution.py:215
  20.2 1.3 %collective-permute-start.9 = (bf16[4,128,128]{2,1,0:T(8,128)(2,1)S(1)}, bf16[4,128,128]{2,1,0:T(8,128)(2,1)S(1)}, u32[]{:S(2)}, u32[]{:S(2)}) collective-permute-start(bf16[4,128,128]{2,1,0:T(8,128)(2,1)S(1)} %collective-permute-done.4.refs_7_), channel_id=1, source_target_pairs={{0,1},{1,0},{2,3},{3,2},{4,5},{5,4},{6,7},{7,6},{8,9},{9,8},{10,11... | collective-permute-start | bytes 393224 | tf_op jit(solution)/shard_map/ppermute | solution.py:215
  28.9 2.0 %collective-permute-start.10 = (bf16[8,2,128,128]{3,2,1,0:T(8,128)(2,1)S(1)}, bf16[8,2,128,128]{3,2,1,0:T(8,128)(2,1)S(1)}, u32[]{:S(2)}, u32[]{:S(2)}) collective-permute-start(bf16[8,2,128,128]{3,2,1,0:T(8,128)(2,1)S(1)} %slice.47), channel_id=1, source_target_pairs={{0,1},{1,0},{2,3},{3,2},{4,5},{5,4},{6,7},{7,6},{8,9},{9,8},{10,11... | collective-permute-start | bytes 1572872 | tf_op jit(solution)/shard_map/ppermute | solution.py:215
  29.1 6.7 %collective-permute-start.13 = (bf16[4,2,128,128]{3,2,1,0:T(8,128)(2,1)S(1)}, bf16[4,2,128,128]{3,2,1,0:T(8,128)(2,1)S(1)}, u32[]{:S(2)}, u32[]{:S(2)}) collective-permute-start(bf16[4,2,128,128]{3,2,1,0:T(8,128)(2,1)S(1)} %slice.51), channel_id=1, source_target_pairs={{0,1},{1,0},{2,3},{3,2},{4,5},{5,4},{6,7},{7,6},{8,9},{9,8},{10,11... | collective-permute-start | bytes 786440 | tf_op jit(solution)/shard_map/ppermute | solution.py:215
  31.0 12.3 %collective-permute-start.12 = (bf16[2,4,128,128]{3,2,0,1:T(8,128)(2,1)S(1)}, bf16[2,4,128,128]{3,2,0,1:T(8,128)(2,1)S(1)}, u32[]{:S(2)}, u32[]{:S(2)}) collective-permute-start(bf16[2,4,128,128]{3,2,0,1:T(8,128)(2,1)S(1)} %get-tuple-element.28), channel_id=1, source_target_pairs={{0,4},{1,5},{2,6},{3,7},{4,8},{5,9},{6,10},{7,11},{8,12},{9,13},{1... | collective-permute-start | bytes 786440 | tf_op jit(solution)/shard_map/ppermute | solution.py:215
  31.8 13.7 %collective-permute-start.11 = (bf16[2,4,128,128]{3,2,0,1:T(8,128)(2,1)S(1)}, bf16[2,4,128,128]{3,2,0,1:T(8,128)(2,1)S(1)}, u32[]{:S(2)}, u32[]{:S(2)}) collective-permute-start(bf16[2,4,128,128]{3,2,0,1:T(8,128)(2,1)S(1)} %get-tuple-element.29), channel_id=1, source_target_pairs={{0,28},{1,29},{2,30},{3,31},{4,0},{5,1},{6,2},{7,3},{8,4},{9,5},{1... | collective-permute-start | bytes 786440 | tf_op jit(solution)/shard_map/ppermute | solution.py:215

commit v4 on v3

--- a/solution.py
+++ b/solution.py
@@ -176,7 +176,7 @@
 
     for row in range(rows):
         for at, turned, mine, mates, part in parts(0, row):
-            add(kept, (0, at), jnp.where(mine, part, 0.0))
+            add(kept, (at, 0), jnp.where(mine, part, 0.0))
             if cores > 1:
                 add(sent, (turned, 0), jnp.where(mates, part, 0.0))
     for i, row, upper, right in strips():
@@ -189,7 +189,7 @@
         full2[upper, right] = value
     for row in range(rows):
         for at, turned, mine, mates, part in parts(1, row):
-            add(kept, (1, at), jnp.where(mine, part, 0.0))
+            add(kept, (at, 1), jnp.where(mine, part, 0.0))
             if cores > 1:
                 add(sent, (turned, 1), jnp.where(mates, part, 0.0))
 
@@ -243,7 +243,7 @@
     kept, sent = pl.pallas_call(
         functools.partial(step_kernel, sizes),
         out_shape=(
-            jax.ShapeDtypeStruct((2, slots, bs, bs), f32),
+            jax.ShapeDtypeStruct((slots, 2, bs, bs), f32),
             jax.ShapeDtypeStruct((slots, 2, bs, bs), bf16),
         ),
         in_specs=[smem] * (2 * groups + 1) + [vmem] * len(blocks),
@@ -260,19 +260,19 @@
         compiler_params=pltpu.CompilerParams(vmem_limit_bytes=24 * 2**20),
         name="submatrix_step",
     )(*ids, *scales, potential, *blocks)
-    kept = [kept[:, i * pieces : (i + 1) * pieces] for i in range(3)]
+    kept = [kept[i * pieces : (i + 1) * pieces] for i in range(3)]
+    mate = [sent[i * pieces : (i + 1) * pieces] for i in range(3)]
     if cores > 1:
-        leaving = jnp.swapaxes(send(sent[: 2 * pieces], same, 0, 1), 0, 1)
-        staying = send(sent[2 * pieces :], same, 0, 1)
-        kept[0] += leaving[:, :pieces].astype(f32)
-        kept[2] += leaving[:, pieces:].astype(f32)
+        mate = [send(part, same, 0, 1) for part in mate]
+        kept[0] = kept[0] + mate[0].astype(f32)
+        kept[2] = lax.optimization_barrier(kept[2]) + mate[1].astype(f32)
     below = send(kept[0].astype(bf16), lambda s: s - 1)
     above = send(kept[2].astype(bf16), lambda s: s + 1)
     last = [below, above]
     if cores > 1:
-        last = lax.optimization_barrier(last + [staying])
-        last[2] = jnp.swapaxes(last[2], 0, 1)
-    return tuple(kept[1][i] + sum(part[i].astype(f32) for part in last) for i in range(2))
+        last = lax.optimization_barrier(last + [mate[2]])
+    total = [kept[1][:, i] + sum(part[:, i].astype(f32) for part in last) for i in range(2)]
+    return tuple(total)
 
 
 def solution(mesh):

time: 46.5 us -> 46.8 us (level)
    ppermute x14 -> x15, waiting for transfers between devices: 15.4 us -> 15.6 us  [send(): return lax.ppermute(value, AXES, pairs)]
    ppermute x14 -> x15, starting transfers between devices: 18.9 us -> 19 us  [send(): return lax.ppermute(value, AXES, pairs)]
  transfers between devices with their start and end apart: 14 -> 15, of which waited for: 7 -> 8; matrix products, arithmetic and copies ran while one was open for 5% -> 5% of each run, Pallas kernels for 0% -> 0%
where the time goes in v4:
time: 46.8 us; the launch traced here: 46.7 us
  starting transfers between devices  19 us (41%)
  waiting for transfers between devices  15.6 us (33%)
  Pallas kernels  7.26 us (16%)
  local copies, waits for them, and re-layouts  2.39 us (5%)
  between operations  1.4 us (3%)
  other arithmetic  1.04 us (2%)
    ppermute x15, starting transfers between devices, send(): return lax.ppermute(value, AXES, pairs)  19 us
    ppermute x15, waiting for transfers between devices, send(): return lax.ppermute(value, AXES, pairs)  15.6 us
    pallas_call x1, Pallas kernels, shards(): pl.pallas_call(functools.partial(step_kernel, sizes), out_shape=(jax.Shap...  7.26 us
    unnamed x3, local copies, waits for them, and re-layouts  0.98 us
  transfers between devices with their start and end apart: 15, of which 8 were waited for; matrix products, arithmetic and copies ran while one was open for 5% of the time, Pallas kernels for 0%

profile of v4, /device:TPU:0, one launch (start us, length us, event | category | flops | bytes accessed | tf_op | source)
XLA Modules:
  0.0 46.7 jit_solution(13821538305324851909)
XLA Ops:
  0.6 3.1 %collective-permute-start = (bf16[4,128,128]{2,1,0:T(8,128)(2,1)}, bf16[4,128,128]{2,1,0:T(8,128)(2,1)S(1)}, u32[]{:S(2)}, u32[]{:S(2)}) collective-permute-start(bf16[4,128,128]{2,1,0:T(8,128)(2,1)} %param.4), channel_id=1, source_target_pairs={{0,4},{1,5},{2,6},{3,7},{4,0},{5,1},{6,2},{7,3},{8,12},{9,13},{10,... | collective-permute-start | bytes 393224 | tf_op jit(solution)/shard_map/ppermute | solution.py:215
  3.7 1.5 %collective-permute-start.1 = (bf16[4,128,128]{2,1,0:T(8,128)(2,1)}, bf16[4,128,128]{2,1,0:T(8,128)(2,1)S(1)}, u32[]{:S(2)}, u32[]{:S(2)}) collective-permute-start(bf16[4,128,128]{2,1,0:T(8,128)(2,1)} %param.4), channel_id=1, source_target_pairs={{0,2},{1,3},{2,0},{3,1},{4,6},{5,7},{6,4},{7,5},{8,10},{9,11},{10,... | collective-permute-start | bytes 393224 | tf_op jit(solution)/shard_map/ppermute | solution.py:215
  5.2 0.0 collective-permute-start.3
  5.2 5.0 %collective-permute-start.2 = (bf16[4,128,128]{2,1,0:T(8,128)(2,1)}, bf16[4,128,128]{2,1,0:T(8,128)(2,1)S(1)}, u32[]{:S(2)}, u32[]{:S(2)}) collective-permute-start(bf16[4,128,128]{2,1,0:T(8,128)(2,1)} %param.4), channel_id=1, source_target_pairs={{0,28},{1,29},{2,30},{3,31},{4,8},{5,9},{6,10},{7,11},{8,4},{9,5},... | collective-permute-start | bytes 393224 | tf_op jit(solution)/shard_map/ppermute | solution.py:215
  10.2 0.9 %constant_dynamic-update-slice_fusion.2 = bf16[12,128,128]{2,1,0:T(8,128)(2,1)S(1)} fusion(bf16[4,128,128]{2,1,0:T(8,128)(2,1)} %param.4), kind=kLoop, calls=%fused_computation.6 | loop fusion | bytes 262144
  11.2 0.0 collective-permute-done
  11.2 0.0 collective-permute-done.1
  11.2 0.1 collective-permute-start.7
  11.3 2.9 %collective-permute-done.2 = bf16[4,128,128]{2,1,0:T(8,128)(2,1)S(1)} collective-permute-done((bf16[4,128,128]{2,1,0:T(8,128)(2,1)}, bf16[4,128,128]{2,1,0:T(8,128)(2,1)S(1)}, u32[]{:S(2)}, u32[]{:S(2)}) %collective-permute-start.2) | collective-permute-done | bytes 131104 | tf_op jit(solution)/shard_map/ppermute | solution.py:215
  14.3 1.6 %collective-permute-start.4 = (bf16[4,128,128]{2,1,0:T(8,128)(2,1)S(1)}, bf16[4,128,128]{2,1,0:T(8,128)(2,1)S(1)}, u32[]{:S(2)}, u32[]{:S(2)}) collective-permute-start(bf16[4,128,128]{2,1,0:T(8,128)(2,1)S(1)} %collective-permute-done.2), channel_id=1, source_target_pairs={{0,2},{1,3},{2,0},{3,1},{4,6},{5,7},{6,4},{7,5},{8,10},{9,11},{10,... | collective-permute-start | bytes 393224 | tf_op jit(solution)/shard_map/ppermute | solution.py:215
  15.9 0.0 collective-permute-done.3
  16.0 0.1 collective-permute-start.8
  16.0 0.5 collective-permute-start.5
  16.5 1.6 %collective-permute-start.6 = (f32[1,10]{1,0:T(1,128)}, f32[1,10]{1,0:T(1,128)S(1)}, u32[]{:S(2)}, u32[]{:S(2)}) collective-permute-start(f32[1,10]{1,0:T(1,128)} %param.6), channel_id=1, source_target_pairs={{0,2},{1,3},{2,0},{3,1},{4,6},{5,7},{6,4},{7,5},{8,10},{9,11},{10,... | collective-permute-start | bytes 128 | tf_op jit(solution)/shard_map/ppermute | solution.py:215
  18.1 0.7 %pad.8.refs_0_ = s32[1,11]{1,0:T(1,128)S(1)} pad(s32[1,10]{1,0:T(1,128)} %param.5, s32[]{:T(128)} %constant.2.clone.1), padding=0_0x0_1 | pad | bytes 88 | tf_op jit(solution)/shard_map/jit(_pad)/pad | solution.py:226
  18.8 0.7 %pad.9.refs_2_ = f32[1,11]{1,0:T(1,128)S(1)} pad(f32[1,10]{1,0:T(1,128)} %param.6, f32[]{:T(128)} %constant.3.clone.1), padding=0_0x0_1 | pad | bytes 88 | tf_op jit(solution)/shard_map/jit(_pad)/pad | solution.py:227
  19.5 0.4 collective-permute-done.5.refs_1_
  19.8 0.4 collective-permute-done.6.refs_3_
  20.2 0.0 collective-permute-done.4.refs_7_
  20.2 0.0 collective-permute-start.9
  20.9 0.0 collective-permute-done.8.refs_9_
  20.9 0.7 %collective-permute-done.9.refs_10_ = bf16[4,128,128]{2,1,0:T(8,128)(2,1)S(1)} collective-permute-done((bf16[4,128,128]{2,1,0:T(8,128)(2,1)S(1)}, bf16[4,128,128]{2,1,0:T(8,128)(2,1)S(1)}, u32[]{:S(2)}, u32[]{:S(2)}) %collective-permute-start.9) | collective-permute-done | bytes 131104 | tf_op jit(solution)/shard_map/ppermute | solution.py:215
  21.5 0.0 collective-permute-done.7.refs_8_
  21.6 7.3 %submatrix_step.1 = (f32[12,2,128,128]{3,2,1,0:T(8,128)S(1)}, bf16[12,2,128,128]{3,2,1,0:T(8,128)(2,1)S(1)}) custom-call(s32[1,11]{1,0:T(1,128)S(1)} %pad.8.refs_0_, s32[1,10]{1,0:T(1,128)S(1)} %collective-permute-done.5.refs_1_, f32[1,11]{1,0:T(1,128)S(1)} %pad.9.refs_2_, f32[1,10]{1,0:T(1,128)S(1)} %collective-permute-done.6.refs_3_, f32[1]{0:T(128)S(6)} %copy.9.refs_4_, ...), custom_call_target="tpu_custom_call" | custom-call | tf_op jit(solution)/shard_map/submatrix_step/pallas_call | solution.py:243
  28.8 0.1 fusion.1
  28.9 0.2 collective-permute-start.10
  29.1 0.4 collective-permute-start.14
  29.5 0.1 collective-permute-start.12
  29.6 0.9 %collective-permute-done.10 = bf16[4,2,128,128]{3,2,1,0:T(8,128)(2,1)S(1)} collective-permute-done((bf16[4,2,128,128]{3,2,1,0:T(8,128)(2,1)S(1)}, bf16[4,2,128,128]{3,2,1,0:T(8,128)(2,1)S(1)}, u32[]{:S(2)}, u32[]{:S(2)}) %collective-permute-start.10) | collective-permute-done | bytes 262176 | tf_op jit(solution)/shard_map/ppermute | solution.py:215
  30.5 0.1 fusion
  30.6 0.7 %collective-permute-done.12 = bf16[4,2,128,128]{3,2,1,0:T(8,128)(2,1)S(1)} collective-permute-done((bf16[4,2,128,128]{3,2,1,0:T(8,128)(2,1)S(1)}, bf16[4,2,128,128]{3,2,1,0:T(8,128)(2,1)S(1)}, u32[]{:S(2)}, u32[]{:S(2)}) %collective-permute-start.12) | collective-permute-done | bytes 262176 | tf_op jit(solution)/shard_map/ppermute | solution.py:215
  31.2 0.1 add_convert_fusion
  31.3 0.8 %collective-permute-start.13 = (bf16[4,2,128,128]{3,2,1,0:T(8,128)(2,1)S(1)}, bf16[4,2,128,128]{3,2,1,0:T(8,128)(2,1)S(1)}, u32[]{:S(2)}, u32[]{:S(2)}) collective-permute-start(bf16[4,2,128,128]{3,2,1,0:T(8,128)(2,1)S(1)} %add_convert_fusion), channel_id=1, source_target_pairs={{0,4},{1,5},{2,6},{3,7},{4,8},{5,9},{6,10},{7,11},{8,12},{9,13},{1... | collective-permute-start | bytes 786440 | tf_op jit(solution)/shard_map/ppermute | solution.py:215
  32.1 4.0 %collective-permute-start.11 = (bf16[4,2,128,128]{3,2,1,0:T(8,128)(2,1)S(1)}, bf16[4,2,128,128]{3,2,1,0:T(8,128)(2,1)S(1)}, u32[]{:S(2)}, u32[]{:S(2)}) collective-permute-start(bf16[4,2,128,128]{3,2,1,0:T(8,128)(2,1)S(1)} %get-tuple-element.29), channel_id=1, source_target_pairs={{0,28},{1,29},{2,30},{3,31},{4,0},{5,1},{6,2},{7,3},{8,4},{9,5},{1... | collective-permute-start | bytes 786440 | tf_op jit(solution)/shard_map/ppermute | solution.py:215
  36.1 0.0 collective-permute-done.14
  36.1 7.5 %collective-permute-done.13 = bf16[4,2,128,128]{3,2,1,0:T(8,128)(2,1)S(1)} collective-permute-done((bf16[4,2,128,128]{3,2,1,0:T(8,128)(2,1)S(1)}, bf16[4,2,128,128]{3,2,1,0:T(8,128)(2,1)S(1)}, u32[]{:S(2)}, u32[]{:S(2)}) %collective-permute-start.13) | collective-permute-done | bytes 262176 | tf_op jit(solution)/shard_map/ppermute | solution.py:215
  43.6 2.2 %collective-permute-done.11 = bf16[4,2,128,128]{3,2,1,0:T(8,128)(2,1)S(1)} collective-permute-done((bf16[4,2,128,128]{3,2,1,0:T(8,128)(2,1)S(1)}, bf16[4,2,128,128]{3,2,1,0:T(8,128)(2,1)S(1)}, u32[]{:S(2)}, u32[]{:S(2)}) %collective-permute-start.11) | collective-permute-done | bytes 262176 | tf_op jit(solution)/shard_map/ppermute | solution.py:215
  45.8 0.9 %add_bitcast_fusion = (f32[4,128,128]{2,1,0:T(8,128)}, f32[4,128,128]{2,1,0:T(8,128)}) fusion(f32[12,2,128,128]{3,2,1,0:T(8,128)S(1)} %get-tuple-element.21, bf16[4,2,128,128]{3,2,1,0:T(8,128)(2,1)S(1)} %collective-permute-done.14, bf16[4,2,128,128]{3,2,1,0:T(8,128)(2,1)S(1)} %collective-permute-done.13, bf16[4,2,128,128]{3,2,1,0:T(8,128)(2,1)S(1)} %collective-permute-done.11), kind=kLoop, calls=%fused_computation.2 | loop fusion | flops 786432 | bytes 1835008 | tf_op jit(solution)/shard_map/add | solution.py:274
  (4 shorter events, 0.1 us)
Async XLA Ops:
  0.6 10.5 %collective-permute-start = (bf16[4,128,128]{2,1,0:T(8,128)(2,1)}, bf16[4,128,128]{2,1,0:T(8,128)(2,1)S(1)}, u32[]{:S(2)}, u32[]{:S(2)}) collective-permute-start(bf16[4,128,128]{2,1,0:T(8,128)(2,1)} %param.4), channel_id=1, source_target_pairs={{0,4},{1,5},{2,6},{3,7},{4,0},{5,1},{6,2},{7,3},{8,12},{9,13},{10,... | collective-permute-start | bytes 393224 | tf_op jit(solution)/shard_map/ppermute | solution.py:215
  3.7 7.5 %collective-permute-start.1 = (bf16[4,128,128]{2,1,0:T(8,128)(2,1)}, bf16[4,128,128]{2,1,0:T(8,128)(2,1)S(1)}, u32[]{:S(2)}, u32[]{:S(2)}) collective-permute-start(bf16[4,128,128]{2,1,0:T(8,128)(2,1)} %param.4), channel_id=1, source_target_pairs={{0,2},{1,3},{2,0},{3,1},{4,6},{5,7},{6,4},{7,5},{8,10},{9,11},{10,... | collective-permute-start | bytes 393224 | tf_op jit(solution)/shard_map/ppermute | solution.py:215
  5.2 10.7 %collective-permute-start.3 = (bf16[4,128,128]{2,1,0:T(8,128)(2,1)}, bf16[4,128,128]{2,1,0:T(8,128)(2,1)S(1)}, u32[]{:S(2)}, u32[]{:S(2)}) collective-permute-start(bf16[4,128,128]{2,1,0:T(8,128)(2,1)} %param.4), channel_id=1, source_target_pairs={{0,6},{1,7},{2,4},{3,5},{4,2},{5,3},{6,0},{7,1},{8,14},{9,15},{10,... | collective-permute-start | bytes 393224 | tf_op jit(solution)/shard_map/ppermute | solution.py:215
  5.2 9.0 %collective-permute-start.2 = (bf16[4,128,128]{2,1,0:T(8,128)(2,1)}, bf16[4,128,128]{2,1,0:T(8,128)(2,1)S(1)}, u32[]{:S(2)}, u32[]{:S(2)}) collective-permute-start(bf16[4,128,128]{2,1,0:T(8,128)(2,1)} %param.4), channel_id=1, source_target_pairs={{0,28},{1,29},{2,30},{3,31},{4,8},{5,9},{6,10},{7,11},{8,4},{9,5},... | collective-permute-start | bytes 393224 | tf_op jit(solution)/shard_map/ppermute | solution.py:215
  11.2 10.3 %collective-permute-start.7 = (bf16[12,128,128]{2,1,0:T(8,128)(2,1)S(1)}, bf16[12,128,128]{2,1,0:T(8,128)(2,1)S(1)}, u32[]{:S(2)}, u32[]{:S(2)}) collective-permute-start(bf16[12,128,128]{2,1,0:T(8,128)(2,1)S(1)} %constant_dynamic-update-slice_fusion.refs_5_), channel_id=1, source_target_pairs={{0,1},{1,0},{2,3},{3,2},{4,5},{5,4},{6,7},{7,6},{8,9},{9,8},{10,11... | collective-permute-start | bytes 1179656 | tf_op jit(solution)/shard_map/ppermute | solution.py:215
  14.3 5.9 %collective-permute-start.4 = (bf16[4,128,128]{2,1,0:T(8,128)(2,1)S(1)}, bf16[4,128,128]{2,1,0:T(8,128)(2,1)S(1)}, u32[]{:S(2)}, u32[]{:S(2)}) collective-permute-start(bf16[4,128,128]{2,1,0:T(8,128)(2,1)S(1)} %collective-permute-done.2), channel_id=1, source_target_pairs={{0,2},{1,3},{2,0},{3,1},{4,6},{5,7},{6,4},{7,5},{8,10},{9,11},{10,... | collective-permute-start | bytes 393224 | tf_op jit(solution)/shard_map/ppermute | solution.py:215
  16.0 4.9 %collective-permute-start.8 = (bf16[8,128,128]{2,1,0:T(8,128)(2,1)S(1)}, bf16[8,128,128]{2,1,0:T(8,128)(2,1)S(1)}, u32[]{:S(2)}, u32[]{:S(2)}) collective-permute-start(bf16[8,128,128]{2,1,0:T(8,128)(2,1)S(1)} %constant_dynamic-update-slice_fusion.3.refs_6_), channel_id=1, source_target_pairs={{0,1},{1,0},{2,3},{3,2},{4,5},{5,4},{6,7},{7,6},{8,9},{9,8},{10,11... | collective-permute-start | bytes 786440 | tf_op jit(solution)/shard_map/ppermute | solution.py:215
  16.0 3.8 %collective-permute-start.5 = (s32[1,10]{1,0:T(1,128)}, s32[1,10]{1,0:T(1,128)S(1)}, u32[]{:S(2)}, u32[]{:S(2)}) collective-permute-start(s32[1,10]{1,0:T(1,128)} %param.5), channel_id=1, source_target_pairs={{0,2},{1,3},{2,0},{3,1},{4,6},{5,7},{6,4},{7,5},{8,10},{9,11},{10,... | collective-permute-start | bytes 128 | tf_op jit(solution)/shard_map/ppermute | solution.py:215
  16.5 3.7 %collective-permute-start.6 = (f32[1,10]{1,0:T(1,128)}, f32[1,10]{1,0:T(1,128)S(1)}, u32[]{:S(2)}, u32[]{:S(2)}) collective-permute-start(f32[1,10]{1,0:T(1,128)} %param.6), channel_id=1, source_target_pairs={{0,2},{1,3},{2,0},{3,1},{4,6},{5,7},{6,4},{7,5},{8,10},{9,11},{10,... | collective-permute-start | bytes 128 | tf_op jit(solution)/shard_map/ppermute | solution.py:215
  20.2 1.3 %collective-permute-start.9 = (bf16[4,128,128]{2,1,0:T(8,128)(2,1)S(1)}, bf16[4,128,128]{2,1,0:T(8,128)(2,1)S(1)}, u32[]{:S(2)}, u32[]{:S(2)}) collective-permute-start(bf16[4,128,128]{2,1,0:T(8,128)(2,1)S(1)} %collective-permute-done.4.refs_7_), channel_id=1, source_target_pairs={{0,1},{1,0},{2,3},{3,2},{4,5},{5,4},{6,7},{7,6},{8,9},{9,8},{10,11... | collective-permute-start | bytes 393224 | tf_op jit(solution)/shard_map/ppermute | solution.py:215
  28.9 1.6 %collective-permute-start.10 = (bf16[4,2,128,128]{3,2,1,0:T(8,128)(2,1)S(1)}, bf16[4,2,128,128]{3,2,1,0:T(8,128)(2,1)S(1)}, u32[]{:S(2)}, u32[]{:S(2)}) collective-permute-start(bf16[4,2,128,128]{3,2,1,0:T(8,128)(2,1)S(1)} %get-tuple-element.32), channel_id=1, source_target_pairs={{0,1},{1,0},{2,3},{3,2},{4,5},{5,4},{6,7},{7,6},{8,9},{9,8},{10,11... | collective-permute-start | bytes 786440 | tf_op jit(solution)/shard_map/ppermute | solution.py:215
  29.1 7.0 %collective-permute-start.14 = (bf16[4,2,128,128]{3,2,1,0:T(8,128)(2,1)S(1)}, bf16[4,2,128,128]{3,2,1,0:T(8,128)(2,1)S(1)}, u32[]{:S(2)}, u32[]{:S(2)}) collective-permute-start(bf16[4,2,128,128]{3,2,1,0:T(8,128)(2,1)S(1)} %get-tuple-element.30), channel_id=1, source_target_pairs={{0,1},{1,0},{2,3},{3,2},{4,5},{5,4},{6,7},{7,6},{8,9},{9,8},{10,11... | collective-permute-start | bytes 786440 | tf_op jit(solution)/shard_map/ppermute | solution.py:215
  29.5 1.8 %collective-permute-start.12 = (bf16[4,2,128,128]{3,2,1,0:T(8,128)(2,1)S(1)}, bf16[4,2,128,128]{3,2,1,0:T(8,128)(2,1)S(1)}, u32[]{:S(2)}, u32[]{:S(2)}) collective-permute-start(bf16[4,2,128,128]{3,2,1,0:T(8,128)(2,1)S(1)} %get-tuple-element.31), channel_id=1, source_target_pairs={{0,1},{1,0},{2,3},{3,2},{4,5},{5,4},{6,7},{7,6},{8,9},{9,8},{10,11... | collective-permute-start | bytes 786440 | tf_op jit(solution)/shard_map/ppermute | solution.py:215
  31.3 12.3 %collective-permute-start.13 = (bf16[4,2,128,128]{3,2,1,0:T(8,128)(2,1)S(1)}, bf16[4,2,128,128]{3,2,1,0:T(8,128)(2,1)S(1)}, u32[]{:S(2)}, u32[]{:S(2)}) collective-permute-start(bf16[4,2,128,128]{3,2,1,0:T(8,128)(2,1)S(1)} %add_convert_fusion), channel_id=1, source_target_pairs={{0,4},{1,5},{2,6},{3,7},{4,8},{5,9},{6,10},{7,11},{8,12},{9,13},{1... | collective-permute-start | bytes 786440 | tf_op jit(solution)/shard_map/ppermute | solution.py:215
  32.1 13.7 %collective-permute-start.11 = (bf16[4,2,128,128]{3,2,1,0:T(8,128)(2,1)S(1)}, bf16[4,2,128,128]{3,2,1,0:T(8,128)(2,1)S(1)}, u32[]{:S(2)}, u32[]{:S(2)}) collective-permute-start(bf16[4,2,128,128]{3,2,1,0:T(8,128)(2,1)S(1)} %get-tuple-element.29), channel_id=1, source_target_pairs={{0,28},{1,29},{2,30},{3,31},{4,0},{5,1},{6,2},{7,3},{8,4},{9,5},{1... | collective-permute-start | bytes 786440 | tf_op jit(solution)/shard_map/ppermute | solution.py:215
